TPU v7x, 8 devices: a whole 2x2x1 slice. The times are simulated.
8 devices in a mesh: dp: 2 (over z, y), cp: 4 (over x, core).
Axes of the slice: x: 2, y: 2, z: 1, core: 2. Of those that a mesh axis runs over, the one named last changes fastest.
Arguments:
- vis_feat: bfloat16 [16, 4096, 1152], P(('dp', 'cp')), parts along dimension 0
- text_emb: bfloat16 [8192, 2048], P(('dp', 'cp')), parts along dimension 0
- img_pos: int32 [16], P('dp'), parts along dimension 0
- grad_y: bfloat16 [8192, 2048], P(('dp', 'cp')), parts along dimension 0
- pn_gain: bfloat16 [1152], replicated
- w_proj: bfloat16 [1152, 2048], replicated
- pre_gain: bfloat16 [2048], replicated
- w_query: bfloat16 [2048, 2048], replicated
- w_key: bfloat16 [2048, 256], replicated
- w_value: bfloat16 [2048, 256], replicated
- q_gain: bfloat16 [256], replicated
- k_gain: bfloat16 [256], replicated
- w_out: bfloat16 [2048, 2048], replicated
- post_gain: bfloat16 [2048], replicated
Outputs:
- output 1: bfloat16 [8192, 2048], P(('dp', 'cp')), parts along dimension 0
- output 2: bfloat16 [8192, 2048], P(('dp', 'cp')), parts along dimension 0
- output 3: bfloat16 [16, 4096, 1152], P(('dp', 'cp')), parts along dimension 0
- output 4: bfloat16 [2304], P('dp'), parts along dimension 0
- output 5: bfloat16 [2304, 2048], P('dp'), parts along dimension 0
- output 6: bfloat16 [4096], P('dp'), parts along dimension 0
- output 7: bfloat16 [4096, 2048], P('dp'), parts along dimension 0
- output 8: bfloat16 [4096, 256], P('dp'), parts along dimension 0
- output 9: bfloat16 [4096, 256], P('dp'), parts along dimension 0
- output 10: bfloat16 [512], P('dp'), parts along dimension 0
- output 11: bfloat16 [512], P('dp'), parts along dimension 0
- output 12: bfloat16 [4096, 2048], P('dp'), parts along dimension 0
- output 13: bfloat16 [4096], P('dp'), parts along dimension 0
There are 2 independent parts. A program takes and returns all parts, laid end to end along the dimension named above; an argument that names none is the same for every part.
All inputs are finite; a program needn't handle non-finite values.
Results may differ from a plain program's by a relative error of at most 0.02.
Values are sent between devices in bfloat16 or wider.
A program may use at most 1 GiB of HBM per device.

v0:
```python
import functools
import jax
import jax.numpy as jnp
from jax import lax
from jax.sharding import PartitionSpec as P

GRID = 64
POOL = 4
EPS = 1e-6
ROPE_BASE = 1000000.0
ROPE_SCALE = 8.0
NEG_BIG = -1e30


def rms_scale(values, gain_vec):
    wide_vals = values.astype(jnp.float32)
    mean_sq = jnp.mean(wide_vals * wide_vals, axis=-1, keepdims=True)
    return wide_vals * lax.rsqrt(mean_sq + EPS) * (1.0 + gain_vec)


def gain_norm(values, gain_vec):
    return rms_scale(values, gain_vec).astype(jnp.bfloat16)


def rope_tables(positions, head_dim):
    inv_freq = ROPE_BASE ** (-jnp.arange(0, head_dim, 2).astype(jnp.float32) / head_dim)
    rot_angle = (positions.astype(jnp.float32) / ROPE_SCALE)[:, None] * inv_freq[None, :]
    rot_angle = jnp.concatenate([rot_angle, rot_angle], axis=-1)
    return jnp.cos(rot_angle)[:, None, :], jnp.sin(rot_angle)[:, None, :]


def apply_rope(values, cos_t, sin_t):
    half_dim = values.shape[-1] // 2
    rotated = jnp.concatenate([-values[..., half_dim:], values[..., :half_dim]], axis=-1)
    return values * cos_t + rotated * sin_t


def qk_rotate(q_raw, k_raw, q_gain, k_gain, cos_t, sin_t):
    q_heads = apply_rope(rms_scale(q_raw, q_gain), cos_t, sin_t).astype(jnp.bfloat16)
    k_heads = apply_rope(rms_scale(k_raw, k_gain), cos_t, sin_t).astype(jnp.bfloat16)
    return q_heads, k_heads


def post_residual(merged, proj_out, gain_vec):
    return (merged.astype(jnp.float32) + rms_scale(proj_out, gain_vec)).astype(jnp.bfloat16)


def pool_patches(vis_loc):
    img_count = vis_loc.shape[0]
    dim_v = vis_loc.shape[2]
    side_len = GRID // POOL
    patch_grid = vis_loc.reshape(img_count, side_len, POOL, side_len, POOL, dim_v)
    pooled = jnp.sum(patch_grid, axis=(2, 4), dtype=jnp.float32) / (POOL * POOL)
    return pooled.astype(jnp.bfloat16).reshape(img_count * side_len * side_len, dim_v)


def unpool_grad(d_pooled, img_count):
    side_len = GRID // POOL
    dim_v = d_pooled.shape[-1]
    spread = (d_pooled.astype(jnp.float32) / (POOL * POOL)).reshape(img_count, side_len, 1, side_len, 1, dim_v)
    spread = jnp.broadcast_to(spread, (img_count, side_len, POOL, side_len, POOL, dim_v))
    return spread.astype(jnp.bfloat16).reshape(img_count, GRID * GRID, dim_v)


def merge_layout(img_pos, dev_rank, seq_loc, block_len):
    q_pos = dev_rank * seq_loc + jnp.arange(seq_loc)
    offset = q_pos[:, None] - img_pos[None, :]
    in_blk = (offset >= 0) & (offset < block_len)
    is_img = jnp.any(in_blk, axis=1)
    flat_row = jnp.sum(jnp.where(in_blk, jnp.arange(img_pos.shape[0])[None, :] * block_len + offset, 0), axis=1)
    blk_start = jnp.where(is_img, q_pos - jnp.sum(jnp.where(in_blk, offset, 0), axis=1), -block_len)
    return q_pos, is_img, flat_row, blk_start


def attn_forward(q_heads, k_all, v_all, visible):
    seq_loc = q_heads.shape[0]
    head_dim = q_heads.shape[-1]
    q_grp = q_heads.reshape(seq_loc, k_all.shape[1], -1, head_dim)
    scores = jnp.einsum('qkgd,skd->kgqs', q_grp, k_all, preferred_element_type=jnp.float32) * head_dim ** -0.5
    probs_hi = jax.nn.softmax(jnp.where(visible, scores, NEG_BIG), axis=-1)
    probs_lo = probs_hi.astype(jnp.bfloat16)
    attn_out = jnp.einsum('kgqs,skd->qkgd', probs_lo, v_all, preferred_element_type=jnp.float32)
    return attn_out.astype(jnp.bfloat16).reshape(seq_loc, -1), probs_hi, probs_lo


def attn_backward(d_attn, q_heads, k_all, v_all, probs_hi, probs_lo):
    seq_loc = q_heads.shape[0]
    head_dim = q_heads.shape[-1]
    q_grp = q_heads.reshape(seq_loc, k_all.shape[1], -1, head_dim)
    d_grp = d_attn.reshape(q_grp.shape)
    d_probs = jnp.einsum('qkgd,skd->kgqs', d_grp, v_all, preferred_element_type=jnp.float32)
    d_v_part = jnp.einsum('kgqs,qkgd->skd', probs_lo, d_grp, preferred_element_type=jnp.float32)
    d_scores = probs_hi * (d_probs - jnp.sum(d_probs * probs_hi, axis=-1, keepdims=True)) * head_dim ** -0.5
    d_scores = d_scores.astype(jnp.bfloat16)
    d_q = jnp.einsum('kgqs,skd->qkgd', d_scores, k_all, preferred_element_type=jnp.float32).astype(jnp.bfloat16).reshape(q_heads.shape)
    d_k_part = jnp.einsum('kgqs,qkgd->skd', d_scores, q_grp, preferred_element_type=jnp.float32)
    return d_q, d_k_part, d_v_part


def solution(mesh):
    group_size = mesh.shape['cp']
    seq_spec = P(('dp', 'cp'))
    part_spec = P('dp')
    rep_spec = P()

    def device_body(vis_loc, text_loc, img_pos, grad_y, pn_gain, w_proj, pre_gain, w_query, w_key, w_value, q_gain, k_gain, w_out, post_gain):
        dev_rank = lax.axis_index('cp')
        seq_loc = text_loc.shape[0]
        img_loc = vis_loc.shape[0]
        head_dim = q_gain.shape[0]
        block_len = (GRID // POOL) ** 2
        pooled = pool_patches(vis_loc)
        normed, norm_pull = jax.vjp(gain_norm, pooled, pn_gain.astype(jnp.float32))
        soft_loc = jnp.dot(normed, w_proj, preferred_element_type=jnp.float32).astype(jnp.bfloat16)
        soft_all = lax.all_gather(soft_loc, 'cp', tiled=True)
        q_pos, is_img, flat_row, blk_start = merge_layout(img_pos, dev_rank, seq_loc, block_len)
        img_mask = is_img[:, None]
        merged = jnp.where(img_mask, jnp.take(soft_all, flat_row, axis=0), text_loc)
        hidden, pre_pull = jax.vjp(gain_norm, merged, pre_gain.astype(jnp.float32))
        q_raw = jnp.dot(hidden, w_query, preferred_element_type=jnp.float32).astype(jnp.bfloat16).reshape(seq_loc, -1, head_dim)
        k_raw = jnp.dot(hidden, w_key, preferred_element_type=jnp.float32).astype(jnp.bfloat16).reshape(seq_loc, -1, head_dim)
        v_loc = jnp.dot(hidden, w_value, preferred_element_type=jnp.float32).astype(jnp.bfloat16).reshape(seq_loc, -1, head_dim)
        cos_t, sin_t = rope_tables(q_pos, head_dim)
        rotate_fn = functools.partial(qk_rotate, cos_t=cos_t, sin_t=sin_t)
        (q_heads, k_loc), qk_pull = jax.vjp(rotate_fn, q_raw, k_raw, q_gain.astype(jnp.float32), k_gain.astype(jnp.float32))
        k_all = lax.all_gather(k_loc, 'cp', tiled=True)
        v_all = lax.all_gather(v_loc, 'cp', tiled=True)
        key_pos = jnp.arange(seq_loc * group_size)
        visible = (key_pos[None, :] <= q_pos[:, None]) | ((key_pos[None, :] >= blk_start[:, None]) & (key_pos[None, :] < blk_start[:, None] + block_len))
        attn_out, probs_hi, probs_lo = attn_forward(q_heads, k_all, v_all, visible)
        proj_out = jnp.dot(attn_out, w_out, preferred_element_type=jnp.float32).astype(jnp.bfloat16)
        y_loc, post_pull = jax.vjp(post_residual, merged, proj_out, post_gain.astype(jnp.float32))
        d_resid, d_proj, g_post = post_pull(grad_y)
        g_out = jnp.einsum('sh,sd->hd', attn_out, d_proj, preferred_element_type=jnp.float32)
        d_attn = jnp.einsum('sd,hd->sh', d_proj, w_out, preferred_element_type=jnp.float32).astype(jnp.bfloat16)
        d_q, d_k_part, d_v_part = attn_backward(d_attn, q_heads, k_all, v_all, probs_hi, probs_lo)
        d_k_loc = lax.psum_scatter(d_k_part, 'cp', scatter_dimension=0, tiled=True).astype(jnp.bfloat16)
        d_v_loc = lax.psum_scatter(d_v_part, 'cp', scatter_dimension=0, tiled=True).astype(jnp.bfloat16)
        d_q_raw, d_k_raw, g_q_gain, g_k_gain = qk_pull((d_q, d_k_loc))
        d_q_flat = d_q_raw.reshape(seq_loc, -1)
        d_k_flat = d_k_raw.reshape(seq_loc, -1)
        d_v_flat = d_v_loc.reshape(seq_loc, -1)
        d_hidden = jnp.einsum('sh,dh->sd', d_q_flat, w_query, preferred_element_type=jnp.float32)
        d_hidden = d_hidden + jnp.einsum('sh,dh->sd', d_k_flat, w_key, preferred_element_type=jnp.float32)
        d_hidden = (d_hidden + jnp.einsum('sh,dh->sd', d_v_flat, w_value, preferred_element_type=jnp.float32)).astype(jnp.bfloat16)
        g_query = jnp.einsum('sd,sh->dh', hidden, d_q_flat, preferred_element_type=jnp.float32)
        g_key = jnp.einsum('sd,sh->dh', hidden, d_k_flat, preferred_element_type=jnp.float32)
        g_value = jnp.einsum('sd,sh->dh', hidden, d_v_flat, preferred_element_type=jnp.float32)
        d_merged_attn, g_pre = pre_pull(d_hidden)
        d_merged = (d_resid.astype(jnp.float32) + d_merged_attn.astype(jnp.float32)).astype(jnp.bfloat16)
        grad_text = jnp.where(img_mask, 0.0, d_merged).astype(jnp.bfloat16)
        d_soft_all = jnp.zeros_like(soft_all).at[flat_row].add(jnp.where(img_mask, d_merged, 0.0).astype(jnp.bfloat16))
        d_soft_loc = lax.psum_scatter(d_soft_all, 'cp', scatter_dimension=0, tiled=True)
        g_proj = jnp.einsum('nc,nd->cd', normed, d_soft_loc, preferred_element_type=jnp.float32)
        d_normed = jnp.einsum('nd,cd->nc', d_soft_loc, w_proj, preferred_element_type=jnp.float32).astype(jnp.bfloat16)
        d_pooled, g_pn = norm_pull(d_normed)
        grad_vis = unpool_grad(d_pooled, img_loc)
        weight_grads = lax.psum((g_pn, g_proj, g_pre, g_query, g_key, g_value, g_q_gain, g_k_gain, g_out, g_post), 'cp')
        return (y_loc, grad_text, grad_vis) + tuple(grad_part.astype(jnp.bfloat16) for grad_part in weight_grads)

    in_specs = (seq_spec, seq_spec, part_spec, seq_spec) + (rep_spec,) * 10
    out_specs = (seq_spec, seq_spec, seq_spec) + (part_spec,) * 10
    return jax.shard_map(device_body, mesh=mesh, in_specs=in_specs, out_specs=out_specs, check_vma=False)
```

profile of v0, /device:TPU:0, one launch (start us, length us, event | category | flops | bytes accessed | tf_op | source)
XLA Modules:
  0.0 1889.6 jit_solution(17829735215170924621)
XLA Ops:
  7.2 34.8 %reshape.468 = f32[2,16,4,16,4,1152]{5,4,3,2,1,0:T(4,128)} reshape(bf16[2,4096,1152]{2,1,0:T(8,128)(2,1)} %param.14) | data formatting | bytes 56623104 | tf_op jit(solution)/shard_map/convert_element_type | solution.py:53
  42.0 15.7 reduce_sum.181
  57.7 2.0 fusion.45
  60.2 1.0 copy-done.30
  61.2 6.5 convolution_convert_fusion.2
  69.3 1.1 fusion.78
  70.5 5.6 fusion.8
  76.0 50.5 %all-gather.6.cloned.1.call-done = bf16[2048,2048]{1,0:T(8,128)(2,1)} async-done(((bf16[512,2048]{1,0:T(8,128)(2,1)}), bf16[2048,2048]{1,0:T(8,128)(2,1)}) %all-gather.6.cloned.1.call-update) | async-done | bytes 8388624 | tf_op jit(solution)/shard_map/all_gather | solution.py:115
  126.5 13.3 gather_fusion
  139.8 4.8 fusion.23
  145.2 1.0 fusion.14
  146.2 1.3 fusion.63
  148.4 5.2 fusion.57
  153.7 11.1 all-gather.8.cloned.1.call-start
  164.8 12.5 convert_convert_fusion
  177.3 7.7 copy.136
  185.0 8.7 copy.112
  193.7 5.4 multiply_reduce_fusion.2
  199.1 1.2 copy.109
  200.3 4.7 multiply_multiply_fusion
  205.1 1.8 slice_negate_fusion.1
  206.9 2.4 copy-done.10
  209.3 4.0 maximum_multiply_fusion
  213.3 9.1 copy.133
  222.4 4.3 mul.466
  226.8 9.2 copy.132
  236.0 4.3 mul.459
  240.2 9.2 copy.131
  249.5 4.2 convolution_convert_fusion.7
  253.8 15.2 add_convert_fusion.2
  269.0 49.9 %fusion.6 = (f32[8,1024]{1,0:T(8,128)S(1)}, f32[4096,1024,8]{1,0,2:T(8,128)}) fusion(pred[1024,4096]{0,1:T(8,128)(4,1)} %fusion.8, bf16[128,8,8,256]{3,2,1,0:T(8,128)(2,1)} %bitcast.216, bf16[4096,256]{0,1:T(8,128)(2,1)} %all-gather.10.cloned.1.call-done), kind=kOutput, calls=%fused_computation.12 | convolution fusion | flops 17280524288 | bytes 144736256 | tf_op jit(solution)/shard_map/qkgd,skd->kgqs/dot_general | solution.py:79
  318.9 42.3 %fusion.5 = f32[8,1024]{1,0:T(8,128)S(1)} fusion(f32[4096,1024,8]{1,0,2:T(8,128)} %get-tuple-element.61, f32[8,1024]{1,0:T(8,128)S(1)} %get-tuple-element.60, pred[1024,4096]{0,1:T(8,128)(4,1)} %fusion.8), kind=kLoop, calls=%fused_computation.11 | loop fusion | flops 134209536 | bytes 138477568 | tf_op jit(solution)/shard_map/reduce_sum | solution.py:80
  361.2 66.6 %convert_bitcast_fusion = bf16[8,1024,4096]{1,2,0:T(8,128)(2,1)} fusion(f32[8,1024]{1,0:T(8,128)S(1)} %fusion.5, f32[8,1024]{1,0:T(8,128)S(1)} %get-tuple-element.60, f32[4096,1024,8]{1,0,2:T(8,128)} %get-tuple-element.61, pred[1024,4096]{0,1:T(8,128)(4,1)} %fusion.8), kind=kLoop, calls=%fused_computation.14 | loop fusion | flops 167772160 | bytes 205586432 | tf_op jit(solution)/shard_map/reshape.9
  427.8 26.9 %convolution_convert_fusion.5 = bf16[256,8,1024]{2,0,1:T(8,128)(2,1)S(1)} fusion(bf16[8,1024,4096]{1,2,0:T(8,128)(2,1)} %convert_bitcast_fusion, bf16[4096,256]{1,0:T(8,128)(2,1)} %all-gather.8.cloned.1.call-done), kind=kOutput, calls=%fused_computation.90 | convolution fusion | flops 17181966336 | bytes 73400320 | tf_op jit(solution)/shard_map/kgqs,skd->qkgd/dot_general | solution.py:82
  454.7 13.6 fusion.21
  468.5 8.4 fusion.17
  476.9 13.1 convolution_convert_fusion
  489.9 99.8 %fusion = (f32[8,1024]{1,0:T(8,128)S(1)}, f32[4096,1024,8]{1,0,2:T(8,128)}) fusion(f32[8,1024]{1,0:T(8,128)S(1)} %fusion.5, f32[8,1024]{1,0:T(8,128)S(1)} %get-tuple-element.60, f32[4096,1024,8]{1,0,2:T(8,128)} %get-tuple-element.61, pred[1024,4096]{0,1:T(8,128)(4,1)} %fusion.8, bf16[128,8,8,256]{3,2,1,0:T(8,128)(2,1)} %bitcast.217, ...), kind=kOutput, calls=%fused_computation.5 | convolution fusion | flops 17381187584 | bytes 279019520 | tf_op jit(solution)/shard_map/qkgd,skd->kgqs/dot_general | solution.py:91
  589.8 105.8 %fusion.7 = bf16[8,1024,4096]{1,2,0:T(8,128)(2,1)} fusion(f32[4096,1024,8]{1,0,2:T(8,128)} %get-tuple-element.65, f32[8,1024]{1,0:T(8,128)S(1)} %get-tuple-element.64, f32[8,1024]{1,0:T(8,128)S(1)} %fusion.5, f32[8,1024]{1,0:T(8,128)S(1)} %get-tuple-element.60, f32[4096,1024,8]{1,0,2:T(8,128)} %get-tuple-element.61, pred[1024,4096]{0,1:T(8,128)(4,1)} %fusion.8), kind=kLoop, calls=%fused_computation.13 | loop fusion | flops 268435456 | bytes 339836928 | tf_op jit(solution)/shard_map/reshape.17
  695.6 33.0 %convolution_bitcast_fusion.1 = f32[4096,1,256]{0,2,1:T(8,128)} fusion(bf16[8,1024,4096]{1,2,0:T(8,128)(2,1)} %fusion.7, f32[1024,8,256]{0,2,1:T(8,128)} %maximum_multiply_fusion, f32[1024,8,256]{0,2,1:T(8,128)} %copy-done.10, f32[1024,256]{0,1:T(8,128)S(1)} %copy-done.12), kind=kOutput, calls=%fused_computation.66 | convolution fusion | flops 17186160640 | bytes 89128960 | tf_op jit(solution)/shard_map/kgqs,qkgd->skd/dot_general | solution.py:96
  728.6 87.3 %copy.123 = bf16[8,1024,4096]{2,0,1:T(8,128)(2,1)} copy(bf16[8,1024,4096]{1,2,0:T(8,128)(2,1)} %convert_bitcast_fusion) | data formatting | bytes 134217728 | tf_op jit(solution)/shard_map/reshape.9
  815.9 5.7 copy.138
  821.6 29.7 %convolution_bitcast_fusion = f32[4096,1,256]{0,2,1:T(8,128)} fusion(bf16[1024,8,256]{2,1,0:T(8,128)(2,1)} %bitcast.219, bf16[8,1024,4096]{2,0,1:T(8,128)(2,1)} %copy.123), kind=kOutput, calls=%fused_computation.65 | convolution fusion | flops 17179869184 | bytes 75497472 | tf_op jit(solution)/shard_map/kgqs,qkgd->skd/dot_general | solution.py:92
  851.4 29.0 %bitcast_multiply_fusion.1 = (f32[1024,8,256]{0,2,1:T(8,128)S(1)}, bf16[256,8,1024]{2,0,1:T(8,128)(2,1)}) fusion(f32[1024,256]{0,1:T(8,128)} %copy-done.4, bf16[8,1024,4096]{1,2,0:T(8,128)(2,1)} %fusion.7, bf16[4096,256]{0,1:T(8,128)(2,1)} %all-gather.10.cloned.1.call-done), kind=kOutput, calls=%fused_computation.54 | convolution fusion | flops 17186160640 | bytes 82837504 | tf_op jit(solution)/shard_map/kgqs,skd->qkgd/dot_general | solution.py:95
  880.5 5.2 fusion.93
  885.8 7.9 multiply_reduce_fusion
  894.8 6.3 fusion.19
  901.1 14.8 fusion.95
  916.0 4.6 convert_multiply_fusion.16
  920.7 5.2 fusion.59
  926.2 4.7 fusion.96
  930.9 9.6 fusion.15
  940.7 5.6 broadcast_select_fusion
  946.4 20.2 %scatter_custom_fusion = bf16[2048,2048]{1,0:T(8,128)(2,1)} fusion(s32[1024]{0:T(1024)} %bitcast.223, bf16[1024,2048]{1,0:T(8,128)(2,1)} %get-tuple-element.36, bf16[]{:T(256)} %constant.44.clone.1, pred[1024]{0:T(1024)(128)(4,1)S(1)} %copy-done.51), kind=kCustom, calls=%fused_computation.75 | custom fusion | flops 4194304 | bytes 12584960 | tf_op jit(solution)/shard_map/scatter-add | solution.py:152
  966.7 16.1 fusion.98
  982.8 12.4 fusion.88
  995.2 2.7 fusion.99
  997.9 2.7 fusion.73
  1000.6 31.3 %reduce-scatter.8.cloned.1.call-done = bf16[512,2048]{1,0:T(8,128)(2,1)} async-done(((bf16[2048,2048]{1,0:T(8,128)(2,1)}), bf16[512,2048]{1,0:T(8,128)(2,1)}) %reduce-scatter.8.cloned.1.call-update) | async-done | bytes 2097168 | tf_op jit(solution)/shard_map/reduce_scatter | solution.py:153
  1031.9 6.2 fusion.44
  1038.8 10.4 broadcast_in_dim.116
  1049.2 29.8 %reshape.467 = bf16[2,4096,1152]{2,1,0:T(8,128)(2,1)} reshape(bf16[2,16,4,16,4,1152]{5,4,3,2,1,0:T(4,128)(2,1)} %broadcast_in_dim.116) | data formatting | bytes 37748736 | tf_op jit(solution)/shard_map/reshape | solution.py:62
  1079.0 8.4 fusion.97
  1087.4 795.1 %all-reduce.6 = (bf16[1152]{0:T(1024)(128)(2,1)}, bf16[1152,2048]{1,0:T(8,128)(2,1)}, bf16[2048]{0:T(1024)(128)(2,1)}, bf16[2048,2048]{1,0:T(8,128)(2,1)}, bf16[...) all-reduce(f32[1152]{0:T(1024)S(1)} %get-tuple-element.19, ...), channel_id=1, replica_groups=mesh['dp'=2,'cp'=4] {'cp'}, use_global_device_ids=true, to_apply=%region_22.23 | all-reduce | flops 11802240 | bytes 70813440 | tf_op jit(solution)/shard_map/psum | solution.py:158
  (199 shorter events, 5.8 us)
Async XLA Ops:
  7.2 242.3 %copy-start = (bf16[2048,256]{1,0:T(8,128)(2,1)S(1)}, bf16[2048,256]{1,0:T(8,128)(2,1)}, u32[]{:S(2)}) copy-start(bf16[2048,256]{1,0:T(8,128)(2,1)} %param.23) | copy-start | bytes 3145732
  7.2 119.3 %all-gather.6.cloned.1.call-start = ((), (), s32[]{:S(2)}) async-start(), calls=%async_computation.3 | async-start | bytes 10485760 | tf_op jit(solution)/shard_map/all_gather | solution.py:115
  42.0 17.7 copy-start.65
  59.7 8.1 copy-start.20
  59.7 8.1 copy-start.41
  59.8 8.0 copy-start.52
  59.8 7.9 copy-start.54
  61.2 7.1 copy-start.70
  61.2 7.4 copy-start.72
  61.2 7.4 copy-start.66
  61.2 7.5 copy-start.67
  67.8 201.2 %all-gather.10.cloned.1.call-start = ((), (), s32[]{:S(2)}) async-start(), calls=%async_computation.8 | async-start | bytes 2621440 | tf_op jit(solution)/shard_map/all_gather | solution.py:126
  68.3 132.0 %copy-start.56 = (f32[256]{0:T(256)}, f32[256]{0:T(256)S(1)}, u32[]{:S(2)}) copy-start(f32[256]{0:T(256)S(1)} %convert_add_fusion.5) | copy-start | bytes 3076
  68.5 71.3 %copy-start.50 = (pred[1024]{0:T(1024)(128)(4,1)}, pred[1024]{0:T(1024)(128)(4,1)S(1)}, u32[]{:S(2)}) copy-start(pred[1024]{0:T(1024)(128)(4,1)S(1)} %fusion.84) | copy-start | bytes 3076
  68.6 79.4 %copy-start.63 = (f32[256]{0:T(256)}, f32[256]{0:T(256)S(1)}, u32[]{:S(2)}) copy-start(f32[256]{0:T(256)S(1)} %convert_add_fusion.6) | copy-start | bytes 3076
  68.7 76.5 %copy-start.37 = (f32[2048]{0:T(1024)}, f32[2048]{0:T(1024)S(1)}, u32[]{:S(2)}) copy-start(f32[2048]{0:T(1024)S(1)} %convert_add_fusion.3) | copy-start | bytes 24580
  146.2 7.4 copy-start.15
  153.6 55.7 %copy-start.4 = (f32[1024,256]{0,1:T(8,128)}, f32[1024,256]{0,1:T(8,128)S(1)}, u32[]{:S(2)}) copy-start(f32[1024,256]{0,1:T(8,128)S(1)} %get-tuple-element.54) | copy-start | bytes 3145732
  153.6 68.8 %copy-start.11 = (f32[1024,256]{0,1:T(8,128)}, f32[1024,256]{0,1:T(8,128)S(1)}, u32[]{:S(2)}) copy-start(f32[1024,256]{0,1:T(8,128)S(1)} %get-tuple-element.55) | copy-start | bytes 3145732
  153.7 274.2 %all-gather.8.cloned.1.call-start = ((), (), s32[]{:S(2)}) async-start(), calls=%async_computation.7 | async-start | bytes 2621440 | tf_op jit(solution)/shard_map/all_gather | solution.py:127
  177.3 7.7 copy-start.9
  200.3 35.6 %copy-start.33 = (f32[1024,8]{0,1:T(8,128)}, f32[1024,8]{0,1:T(8,128)S(1)}, u32[]{:S(2)}) copy-start(f32[1024,8]{0,1:T(8,128)S(1)} %fusion.83) | copy-start | bytes 98308
  253.7 662.2 %reduce-scatter.4.cloned.1.call-start = ((), (), s32[]{:S(2)}) async-start(), calls=%async_computation.4 | async-start | bytes 5242880 | tf_op jit(solution)/shard_map/reduce_scatter | solution.py:137
  454.7 13.7 copy-start.2
  454.7 13.7 copy-start.6
  454.7 13.7 copy-start.17
  454.7 13.7 copy-start.48
  468.4 8.5 copy-start.26
  468.4 8.4 copy-start.58
  476.9 13.1 copy-start.68
  589.7 105.8 %copy-start.12 = (f32[1024,256]{0,1:T(8,128)S(1)}, f32[1024,256]{0,1:T(8,128)}, u32[]{:S(2)}) copy-start(f32[1024,256]{0,1:T(8,128)} %copy-done.11) | copy-start | bytes 3145732
  728.6 202.3 %reduce-scatter.6.cloned.1.call-start = ((), (), s32[]{:S(2)}) async-start(), calls=%async_computation.5 | async-start | bytes 5242880 | tf_op jit(solution)/shard_map/reduce_scatter | solution.py:138
  851.3 180.5 %reduce-scatter.8.cloned.1.call-start = ((), (), s32[]{:S(2)}) async-start(), calls=%async_computation.6 | async-start | bytes 10485760 | tf_op jit(solution)/shard_map/reduce_scatter | solution.py:153
  880.4 13.3 slice-start
  885.7 8.0 copy-start.36
  885.7 8.0 slice-start.1
  885.7 8.9 copy-start.8
  885.7 9.1 copy-start.14
  901.1 14.9 copy-start.25
  901.1 19.6 %copy-start.24 = (bf16[1024,256]{0,1:T(8,128)(2,1)S(1)}, bf16[1024,256]{0,1:T(8,128)(2,1)}, u32[]{:S(2)}) copy-start(bf16[1024,256]{0,1:T(8,128)(2,1)} %copy-done.23) | copy-start | bytes 1572868
  901.1 19.6 %copy-start.40 = (f32[1024]{0:T(1024)S(1)}, f32[1024]{0:T(1024)}, u32[]{:S(2)}) copy-start(f32[1024]{0:T(1024)} %copy-done.39) | copy-start | bytes 12292
  901.1 19.6 %copy-start.64 = (f32[256]{0:T(256)S(1)}, f32[256]{0:T(256)}, u32[]{:S(2)}) copy-start(f32[256]{0:T(256)} %copy-done.63) | copy-start | bytes 3076
  915.9 9.9 copy-start.61
  915.9 10.2 copy-start.32
  920.7 10.2 copy-start.38
  920.7 10.2 copy-start.44
  930.9 9.7 copy-start.46
  930.9 9.7 copy-start.51
  930.9 9.7 copy-start.7
  930.9 9.8 copy-start.18
  966.6 16.1 copy-start.3
  966.6 16.1 copy-start.19
  966.6 16.1 copy-start.27
  966.6 16.1 copy-start.49
  966.6 16.1 copy-start.59
  966.7 16.1 copy-start.69
  982.8 12.5 copy-start.16
  982.8 15.1 copy-start.28
  995.2 36.7 %copy-start.21 = (bf16[2,16,16,1152]{3,2,1,0:T(8,128)(2,1)S(1)}, bf16[2,16,16,1152]{3,2,1,0:T(8,128)(2,1)}, u32[]{:S(2)}) copy-start(bf16[2,16,16,1152]{3,2,1,0:T(8,128)(2,1)} %copy-done.20) | copy-start | bytes 3538948
  995.2 36.7 %copy-start.42 = (f32[1152]{0:T(1024)S(1)}, f32[1152]{0:T(1024)}, u32[]{:S(2)}) copy-start(f32[1152]{0:T(1024)} %copy-done.41) | copy-start | bytes 13828
  995.2 36.7 %copy-start.55 = (f32[512]{0:T(512)S(1)}, f32[512]{0:T(512)}, u32[]{:S(2)}) copy-start(f32[512]{0:T(512)} %copy-done.54) | copy-start | bytes 6148
  1000.6 37.5 %copy-start.53 = (f32[512]{0:T(512)S(1)}, f32[512]{0:T(512)}, u32[]{:S(2)}) copy-start(f32[512]{0:T(512)} %copy-done.52) | copy-start | bytes 6148
  1079.0 8.4 copy-start.22
  1079.0 8.4 copy-start.47
  (17 other events, 66.2 us)
Sparse Core Ops, SparseCore 0:
  67.9 58.5 all-gather.5
  153.8 19.5 all-gather.9
  253.9 19.5 all-gather.7
  728.7 38.2 reduce-scatter.3
  851.5 38.2 reduce-scatter.5
  966.7 65.1 reduce-scatter.7
where the time goes:
time: 1900 us; the launch traced here: 1890 us
  blocking collectives  795 us (42%)
  matrix products  397 us (21%)
  other arithmetic  347 us (18%)
  local copies, waits for them, and re-layouts  241 us (13%)
  waiting for transfers between devices  81.9 us (4%)
    psum x1, blocking collectives, device_body(): lax.psum((g_pn, g_proj, g_pre, g_query, g_key, g_value, g_q_gain, g_k_gai...  795 us
    another operation x2, other arithmetic  172 us
    dot_general x1, matrix products, attn_backward(): jnp.einsum('qkgd,skd->kgqs', d_grp, v_all, preferred_element_type=jnp.flo...  99.8 us
    another operation x1, local copies, waits for them, and re-layouts  87.3 us
    all_gather x1, waiting for transfers between devices, device_body(): soft_all = lax.all_gather(soft_loc, 'cp', tiled=True)  50.5 us
    dot_general x1, matrix products, attn_forward(): jnp.einsum('qkgd,skd->kgqs', q_grp, k_all, preferred_element_type=jnp.flo...  49.9 us
    reduce_sum x1, other arithmetic, attn_forward(): probs_hi = jax.nn.softmax(jnp.where(visible, scores, NEG_BIG), axis=-1)  42.3 us
  transfers between devices with their start and end apart: 6, of which 2 were waited for; matrix products, arithmetic and copies ran while one was open for 27% of the time, Pallas kernels for 0%

commit v1 on v0

v1 whole, which is shorter than its diff:
```python
import functools
import jax
import jax.numpy as jnp
from jax import lax
from jax.experimental import pallas as pl
from jax.experimental.pallas import tpu as pltpu
from jax.sharding import PartitionSpec as P

GRID = 64
POOL = 4
SIDE = GRID // POOL
BLOCK = SIDE * SIDE
EPS = 1e-6
ROPE_BASE = 1000000.0
ROPE_SCALE = 8.0
NEG_BIG = -1e30
HEAD = 256
HALF = HEAD // 2
BQ = 512
BK = 512
BM = 256
RB = 256
VMEM_LIMIT = 60 * 1024 * 1024
F32 = jnp.float32
BF16 = jnp.bfloat16


def params(sem):
    return pltpu.CompilerParams(dimension_semantics=sem, vmem_limit_bytes=VMEM_LIMIT)


def cost(flops, nbytes):
    return pl.CostEstimate(flops=int(flops), bytes_accessed=int(nbytes), transcendentals=0)


def dot(a, b):
    return jnp.dot(a, b, preferred_element_type=F32)


def dot_t(a, b):
    return lax.dot_general(a, b, (((1,), (1,)), ((), ())), preferred_element_type=F32)


def iota(shape, axis):
    return lax.broadcasted_iota(jnp.int32, shape, axis)


def wide(stat, width):
    return jnp.concatenate([stat] * (width // 128), axis=1)


def pool_kernel(vis_ref, out_ref):
    rows, cols = SIDE, POOL * GRID
    patch = iota((rows, cols), 1) % GRID
    sel = (patch // POOL == iota((rows, cols), 0)).astype(BF16)
    for i in range(vis_ref.shape[1] // cols):
        total = dot(sel, vis_ref[0, i * cols:(i + 1) * cols, :])
        out_ref[i * rows:(i + 1) * rows, :] = (total / (POOL * POOL)).astype(BF16)


def pool_patches(vis_loc):
    n_img, n_patch, dim = vis_loc.shape
    bands = 4
    steps = SIDE // bands
    return pl.pallas_call(
        pool_kernel,
        out_shape=jax.ShapeDtypeStruct((n_img * BLOCK, dim), BF16),
        grid=(n_img, steps),
        in_specs=[pl.BlockSpec((1, bands * POOL * GRID, dim), lambda n, i: (n, i, 0))],
        out_specs=pl.BlockSpec((bands * SIDE, dim), lambda n, i: (n * steps + i, 0)),
        compiler_params=params(("arbitrary", "arbitrary")),
        cost_estimate=cost(4e9, n_img * n_patch * dim * 2),
        name="pool",
    )(vis_loc)


def unpool_kernel(d_ref, out_ref):
    rows, cols = POOL * GRID, SIDE
    patch = iota((rows, cols), 0) % GRID
    sel = (patch // POOL == iota((rows, cols), 1)).astype(BF16)
    for i in range(out_ref.shape[1] // rows):
        band = (d_ref[i * cols:(i + 1) * cols, :].astype(F32) / (POOL * POOL)).astype(BF16)
        out_ref[0, i * rows:(i + 1) * rows, :] = dot(sel, band).astype(BF16)


def unpool_grad(d_pooled, n_img):
    dim = d_pooled.shape[1]
    bands = 4
    steps = SIDE // bands
    return pl.pallas_call(
        unpool_kernel,
        out_shape=jax.ShapeDtypeStruct((n_img, GRID * GRID, dim), BF16),
        grid=(n_img, steps),
        in_specs=[pl.BlockSpec((bands * SIDE, dim), lambda n, i: (n * steps + i, 0))],
        out_specs=pl.BlockSpec((1, bands * POOL * GRID, dim), lambda n, i: (n, i, 0)),
        compiler_params=params(("arbitrary", "arbitrary")),
        cost_estimate=cost(4e9, n_img * GRID * GRID * dim * 2),
        name="unpool",
    )(d_pooled)


def rms(x):
    return lax.rsqrt(jnp.mean(x * x, axis=-1, keepdims=True) + EPS)


def norm_rope(raw, gain1, cos_t, sin_t):
    x = raw.astype(F32)
    x = x * rms(x) * gain1
    lo, hi = x[:, :HALF], x[:, HALF:]
    return (lo * cos_t - hi * sin_t).astype(BF16), (hi * cos_t + lo * sin_t).astype(BF16)


def norm_rope_grad(d_out, raw, gain1, cos_t, sin_t):
    d = d_out.astype(F32)
    lo, hi = d[:, :HALF], d[:, HALF:]
    d = jnp.concatenate([lo * cos_t + hi * sin_t, hi * cos_t - lo * sin_t], axis=1)
    x = raw.astype(F32)
    r = rms(x)
    xr = x * r
    dg = d * gain1
    d_raw = r * (dg - xr * jnp.mean(xr * dg, axis=-1, keepdims=True))
    return d_raw.astype(BF16), jnp.sum(d * xr, axis=0, keepdims=True)


def qkv_kernel(meta, text_own, text_mate, soft_a, soft_b, pre1, wq, wk, wv, qg1, kg1, cos_ref, sin_ref,
               x_out, hid_out, qraw_out, q_out, kraw_out, k_out, v_out, x_scr):
    i = pl.program_id(0)
    half = pl.num_programs(0) // 2
    own = (i < half) == (meta[0, 0] == 1)

    @pl.when(own)
    def _():
        x_scr[...] = text_own[...]

    @pl.when(jnp.logical_not(own))
    def _():
        x_scr[...] = text_mate[...]

    for slot, soft in ((0, soft_a), (1, soft_b)):
        off = meta[3 + slot, i]

        @pl.when(off < RB)
        def _():
            src = iota((RB, BLOCK), 0) - off
            pick = (src == iota((RB, BLOCK), 1)).astype(BF16)
            row = iota((RB, 1), 0) - off
            inside = (row >= 0) & (row < BLOCK)
            x_scr[...] = jnp.where(inside, dot(pick, soft[...]).astype(BF16), x_scr[...])

    x_out[...] = x_scr[...]
    x = x_scr[...].astype(F32)
    hid_out[...] = (x * rms(x) * pre1[...]).astype(BF16)
    hid = hid_out[...]
    qraw_out[...] = dot(hid, wq[...]).astype(BF16)
    kraw_out[...] = dot(hid, wk[...]).astype(BF16)
    v_out[...] = dot(hid, wv[...]).astype(BF16)
    cos_t, sin_t = cos_ref[...], sin_ref[...]
    lo, hi = norm_rope(kraw_out[...], kg1[...], cos_t, sin_t)
    k_out[:, :HALF] = lo
    k_out[:, HALF:] = hi
    for h in range(q_out.shape[1] // HEAD):
        lo, hi = norm_rope(qraw_out[:, h * HEAD:(h + 1) * HEAD], qg1[...], cos_t, sin_t)
        q_out[:, h * HEAD:h * HEAD + HALF] = (lo * 0.0625).astype(BF16)
        q_out[:, h * HEAD + HALF:(h + 1) * HEAD] = (hi * 0.0625).astype(BF16)


def qkv_call(meta, text_own, text_mate, soft_all, pre1, wq, wk, wv, qg1, kg1, cos_t, sin_t):
    rows, dim = text_own.shape
    steps = 2 * rows // RB
    half = steps // 2
    width = wq.shape[1]

    def own_map(i, meta):
        is_lo = meta[0, 0] == 1
        return jnp.where(is_lo, jnp.minimum(i, half - 1), jnp.maximum(i - half, 0)), 0

    def mate_map(i, meta):
        is_lo = meta[0, 0] == 1
        return jnp.where(is_lo, jnp.maximum(i - half, 0), jnp.minimum(i, half - 1)), 0

    def row(w):
        return pl.BlockSpec((RB, w), lambda i, meta: (i, 0))

    def whole(a):
        return pl.BlockSpec(a.shape, lambda i, meta: (0,) * a.ndim, pipeline_mode=pl.Buffered(1))

    def struct(w):
        return jax.ShapeDtypeStruct((2 * rows, w), BF16)

    return pl.pallas_call(
        qkv_kernel,
        out_shape=[struct(dim), struct(dim), struct(width), struct(width), struct(HEAD), struct(HEAD), struct(HEAD)],
        grid_spec=pltpu.PrefetchScalarGridSpec(
            num_scalar_prefetch=1, grid=(steps,),
            in_specs=[pl.BlockSpec((RB, dim), own_map), pl.BlockSpec((RB, dim), mate_map),
                      pl.BlockSpec((BLOCK, dim), lambda i, meta: (meta[1, i], 0)),
                      pl.BlockSpec((BLOCK, dim), lambda i, meta: (meta[2, i], 0)),
                      whole(pre1), whole(wq), whole(wk), whole(wv), whole(qg1), whole(kg1), row(HALF), row(HALF)],
            out_specs=[row(dim), row(dim), row(width), row(width), row(HEAD), row(HEAD), row(HEAD)],
            scratch_shapes=[pltpu.VMEM((RB, dim), BF16)]),
        compiler_params=params(("arbitrary",)),
        cost_estimate=cost(4 * rows * dim * (width + 2 * HEAD), 60e6),
        name="qkv",
    )(meta, text_own, text_mate, soft_all, soft_all, pre1, wq, wk, wv, qg1, kg1, cos_t, sin_t)


def fwd_kernel(span, q_ref, kt_ref, v_ref, lim_ref, o_ref, lse_ref, acc, m_scr, l_scr):
    b = pl.program_id(0)
    q = q_ref[...]
    acc[...] = jnp.zeros_like(acc)
    m_scr[...] = jnp.full_like(m_scr, NEG_BIG)
    l_scr[...] = jnp.zeros_like(l_scr)

    def step(off, bk, masked):
        off = pl.multiple_of(off, bk)
        s = dot(q, kt_ref[:, pl.ds(off, bk)])
        if masked:
            key = off + iota(s.shape, 1)
            s = jnp.where(key < wide(lim_ref[...], bk), s, NEG_BIG)
        m_old = m_scr[...]
        m_new = jnp.maximum(m_old, jnp.max(s, axis=1, keepdims=True))
        p = jnp.exp(s - wide(m_new, bk))
        alpha = jnp.exp(m_old - m_new)
        l_scr[...] = alpha * l_scr[...] + jnp.sum(p, axis=1, keepdims=True)
        m_scr[...] = m_new
        acc[...] = acc[...] * wide(alpha, HEAD) + dot(p.astype(BF16), v_ref[pl.ds(off, bk), :])

    @pl.loop(0, span[0, b])
    def _(j):
        step(j * BK, BK, False)

    @pl.loop(span[1, b], span[2, b])
    def _(j):
        step(j * BM, BM, True)

    l = l_scr[...]
    o_ref[...] = (acc[...] / wide(l, HEAD)).astype(BF16)
    lse_ref[0] = (m_scr[...] + jnp.log(l)).T[0:1, :]


def fwd_call(span, q, kt, v, lim):
    rows, width = q.shape
    heads = width // HEAD
    seq = v.shape[0]
    return pl.pallas_call(
        fwd_kernel,
        out_shape=[jax.ShapeDtypeStruct((rows, width), BF16), jax.ShapeDtypeStruct((heads, 1, rows), F32)],
        grid_spec=pltpu.PrefetchScalarGridSpec(
            num_scalar_prefetch=1, grid=(rows // BQ, heads),
            in_specs=[pl.BlockSpec((BQ, HEAD), lambda b, h, s: (b, h)),
                      pl.BlockSpec((HEAD, seq), lambda b, h, s: (0, 0)),
                      pl.BlockSpec((seq, HEAD), lambda b, h, s: (0, 0)),
                      pl.BlockSpec((BQ, 128), lambda b, h, s: (b, 0))],
            out_specs=[pl.BlockSpec((BQ, HEAD), lambda b, h, s: (b, h)),
                       pl.BlockSpec((1, 1, BQ), lambda b, h, s: (h, 0, b))],
            scratch_shapes=[pltpu.VMEM((BQ, HEAD), F32), pltpu.VMEM((BQ, 128), F32), pltpu.VMEM((BQ, 128), F32)]),
        compiler_params=params(("arbitrary", "arbitrary")),
        cost_estimate=cost(2 * rows * seq * width, 30e6),
        name="attn_fwd",
    )(span, q, kt, v, lim)


def bwd_kernel(span, q_ref, do_ref, k_ref, kt_ref, v_ref, lim_ref, lse_ref, delta_ref, qraw_ref, qg1, cos_ref, sin_ref,
               dqraw_ref, gq_ref, dk_ref, dv_ref, qt, dot_scr, dqt):
    b, h = pl.program_id(0), pl.program_id(1)

    @pl.when((b == 0) & (h == 0))
    def _():
        dk_ref[...] = jnp.zeros_like(dk_ref)
        dv_ref[...] = jnp.zeros_like(dv_ref)
        gq_ref[...] = jnp.zeros_like(gq_ref)

    qt[...] = q_ref[...].astype(F32).T.astype(BF16)
    dot_scr[...] = do_ref[...].astype(F32).T.astype(BF16)
    dqt[...] = jnp.zeros_like(dqt)
    lse = lse_ref[0]
    delta = delta_ref[0]

    def step(off, bk, masked):
        off = pl.multiple_of(off, bk)
        rows = pl.ds(off, bk)
        p = jnp.exp(dot(k_ref[rows, :], qt[...]) - lse)
        if masked:
            p = jnp.where(off + iota(p.shape, 0) < lim_ref[...], p, 0.0)
        ds = (p * (dot(v_ref[rows, :], dot_scr[...]) - delta)).astype(BF16)
        dv_ref[rows, :] += dot(p.astype(BF16), do_ref[...])
        dk_ref[rows, :] += dot(ds, q_ref[...])
        dqt[...] += dot(kt_ref[:, rows], ds)

    @pl.loop(0, span[0, b])
    def _(j):
        step(j * BK, BK, False)

    @pl.loop(span[1, b], span[2, b])
    def _(j):
        step(j * BM, BM, True)

    d_q = (dqt[...].T * 0.0625).astype(BF16)
    d_raw, g_part = norm_rope_grad(d_q, qraw_ref[...], qg1[...], cos_ref[...], sin_ref[...])
    dqraw_ref[...] = d_raw
    gq_ref[...] += g_part


def bwd_call(span, q, d_o, k, kt, v, lim_t, lse, delta, q_raw, qg1, cos_t, sin_t):
    rows, width = q.shape
    heads = width // HEAD
    seq = v.shape[0]
    tile = pl.BlockSpec((BQ, HEAD), lambda b, h, s: (b, h))
    keys = pl.BlockSpec((seq, HEAD), lambda b, h, s: (0, 0))
    stat = pl.BlockSpec((1, 1, BQ), lambda b, h, s: (h, 0, b))
    rot = pl.BlockSpec((BQ, HALF), lambda b, h, s: (b, 0))
    return pl.pallas_call(
        bwd_kernel,
        out_shape=[jax.ShapeDtypeStruct((rows, width), BF16), jax.ShapeDtypeStruct((1, HEAD), F32),
                   jax.ShapeDtypeStruct((seq, HEAD), F32), jax.ShapeDtypeStruct((seq, HEAD), F32)],
        grid_spec=pltpu.PrefetchScalarGridSpec(
            num_scalar_prefetch=1, grid=(rows // BQ, heads),
            in_specs=[tile, tile, keys, pl.BlockSpec((HEAD, seq), lambda b, h, s: (0, 0)), keys,
                      pl.BlockSpec((1, BQ), lambda b, h, s: (0, b)), stat, stat, tile,
                      pl.BlockSpec((1, HEAD), lambda b, h, s: (0, 0)), rot, rot],
            out_specs=[tile, pl.BlockSpec((1, HEAD), lambda b, h, s: (0, 0)), keys, keys],
            scratch_shapes=[pltpu.VMEM((HEAD, BQ), BF16), pltpu.VMEM((HEAD, BQ), BF16), pltpu.VMEM((HEAD, BQ), F32)]),
        compiler_params=params(("arbitrary", "arbitrary")),
        cost_estimate=cost(5 * rows * seq * width, 50e6),
        name="attn_bwd",
    )(span, q, d_o, k, kt, v, lim_t, lse, delta, q_raw, qg1, cos_t, sin_t)


def out_kernel(meta, o_ref, x_ref, dy_own, dy_mate, wo, post1, y_ref, da_ref, do_ref, delta_ref, gpost_ref, dy_scr):
    i = pl.program_id(0)
    half = pl.num_programs(0) // 2
    own = (i < half) == (meta[0, 0] == 1)

    @pl.when(i == 0)
    def _():
        gpost_ref[...] = jnp.zeros_like(gpost_ref)

    @pl.when(own)
    def _():
        dy_scr[...] = dy_own[...]

    @pl.when(jnp.logical_not(own))
    def _():
        dy_scr[...] = dy_mate[...]

    a = dot(o_ref[...], wo[...]).astype(BF16).astype(F32)
    r = rms(a)
    ar = a * r

    @pl.when(own)
    def _():
        y_ref[...] = (x_ref[...].astype(F32) + ar * post1[...]).astype(BF16)

    dy = dy_scr[...].astype(F32)
    gpost_ref[...] += jnp.sum(dy * ar, axis=0, keepdims=True)
    dg = dy * post1[...]
    da_ref[...] = (r * (dg - ar * jnp.mean(ar * dg, axis=-1, keepdims=True))).astype(BF16)
    do_ref[...] = dot_t(da_ref[...], wo[...]).astype(BF16)
    cols = []
    for h in range(o_ref.shape[1] // HEAD):
        c = slice(h * HEAD, (h + 1) * HEAD)
        cols.append(jnp.sum(do_ref[:, c].astype(F32) * o_ref[:, c].astype(F32), axis=-1, keepdims=True))
    delta_ref[...] = jnp.concatenate(cols, axis=1)


def own_maps(half):
    def own_map(i, meta):
        is_lo = meta[0, 0] == 1
        return jnp.where(is_lo, jnp.minimum(i, half - 1), jnp.maximum(i - half, 0)), 0

    def mate_map(i, meta):
        is_lo = meta[0, 0] == 1
        return jnp.where(is_lo, jnp.maximum(i - half, 0), jnp.minimum(i, half - 1)), 0

    return own_map, mate_map


def out_call(meta, o, x, dy_own, dy_mate, wo, post1):
    rows, width = o.shape
    dim = wo.shape[1]
    steps = rows // RB
    own_map, mate_map = own_maps(steps // 2)
    row = lambda w: pl.BlockSpec((RB, w), lambda i, meta: (i, 0))
    heads = width // HEAD
    return pl.pallas_call(
        out_kernel,
        out_shape=[jax.ShapeDtypeStruct(dy_own.shape, BF16), jax.ShapeDtypeStruct((rows, dim), BF16),
                   jax.ShapeDtypeStruct((rows, width), BF16), jax.ShapeDtypeStruct((rows, heads), F32),
                   jax.ShapeDtypeStruct((1, dim), F32)],
        grid_spec=pltpu.PrefetchScalarGridSpec(
            num_scalar_prefetch=1, grid=(steps,),
            in_specs=[row(width), row(dim), pl.BlockSpec((RB, dim), own_map), pl.BlockSpec((RB, dim), mate_map),
                      pl.BlockSpec(wo.shape, lambda i, meta: (0, 0), pipeline_mode=pl.Buffered(1)),
                      pl.BlockSpec((1, dim), lambda i, meta: (0, 0))],
            out_specs=[pl.BlockSpec((RB, dim), own_map), row(dim), row(width), row(heads),
                       pl.BlockSpec((1, dim), lambda i, meta: (0, 0))],
            scratch_shapes=[pltpu.VMEM((RB, dim), BF16)]),
        compiler_params=params(("arbitrary",)),
        cost_estimate=cost(4 * rows * dim * width, 60e6),
        name="out_proj",
    )(meta, o, x, dy_own, dy_mate, wo, post1)


def hid_kernel(meta, dq_ref, dk_mine, dv_mine, dkv_theirs, kraw_ref, cos_ref, sin_ref, kg1, wq, wk, wv, x_ref, pre1,
               dy_own, dy_mate, lim_ref, dtext_ref, dm_ref, dk_ref, dv_ref, gpre_ref, gk_ref, dy_scr):
    i = pl.program_id(0)
    half = pl.num_programs(0) // 2
    own = (i < half) == (meta[0, 0] == 1)

    @pl.when(i == 0)
    def _():
        gpre_ref[...] = jnp.zeros_like(gpre_ref)
        gk_ref[...] = jnp.zeros_like(gk_ref)

    @pl.when(own)
    def _():
        dy_scr[...] = dy_own[...]

    @pl.when(jnp.logical_not(own))
    def _():
        dy_scr[...] = dy_mate[...]

    d_k = (dk_mine[...] + dkv_theirs[:, :HEAD]).astype(BF16)
    dv_ref[...] = (dv_mine[...] + dkv_theirs[:, HEAD:]).astype(BF16)
    dk_ref[...], g_part = norm_rope_grad(d_k, kraw_ref[...], kg1[...], cos_ref[...], sin_ref[...])
    gk_ref[...] += g_part
    dh = dot_t(dq_ref[...], wq[...]) + dot_t(dk_ref[...], wk[...]) + dot_t(dv_ref[...], wv[...])
    dh = dh.astype(BF16).astype(F32)
    x = x_ref[...].astype(F32)
    r = rms(x)
    xr = x * r
    gpre_ref[...] += jnp.sum(dh * xr, axis=0, keepdims=True)
    dg = dh * pre1[...]
    dx = (r * (dg - xr * jnp.mean(xr * dg, axis=-1, keepdims=True))).astype(BF16).astype(F32)
    dm = (dy_scr[...].astype(F32) + dx).astype(BF16)
    dm_ref[...] = dm

    @pl.when(own)
    def _():
        dtext_ref[...] = jnp.where(lim_ref[:, :1] > 0, jnp.zeros_like(dm), dm)


def hid_call(meta, dq, dk_part, dv_part, dkv_theirs, k_raw, cos_t, sin_t, kg1, wq, wk, wv, x, pre1, dy_own, dy_mate, img_flag):
    rows, width = dq.shape
    dim = wq.shape[0]
    steps = rows // RB
    own_map, mate_map = own_maps(steps // 2)
    row = lambda w: pl.BlockSpec((RB, w), lambda i, meta: (i, 0))
    part = pl.BlockSpec((RB, HEAD), lambda i, meta: (meta[5, i], 0))
    whole = lambda a: pl.BlockSpec(a.shape, lambda i, meta: (0, 0), pipeline_mode=pl.Buffered(1))
    return pl.pallas_call(
        hid_kernel,
        out_shape=[jax.ShapeDtypeStruct(dy_own.shape, BF16), jax.ShapeDtypeStruct((rows, dim), BF16),
                   jax.ShapeDtypeStruct((rows, HEAD), BF16), jax.ShapeDtypeStruct((rows, HEAD), BF16),
                   jax.ShapeDtypeStruct((1, dim), F32), jax.ShapeDtypeStruct((1, HEAD), F32)],
        grid_spec=pltpu.PrefetchScalarGridSpec(
            num_scalar_prefetch=1, grid=(steps,),
            in_specs=[row(width), part, part, row(2 * HEAD), row(HEAD), row(HALF), row(HALF), whole(kg1),
                      whole(wq), whole(wk), whole(wv), row(dim), whole(pre1),
                      pl.BlockSpec((RB, dim), own_map), pl.BlockSpec((RB, dim), mate_map), row(128)],
            out_specs=[pl.BlockSpec((RB, dim), own_map), row(dim), row(HEAD), row(HEAD),
                       pl.BlockSpec((1, dim), lambda i, meta: (0, 0)), pl.BlockSpec((1, HEAD), lambda i, meta: (0, 0))],
            scratch_shapes=[pltpu.VMEM((RB, dim), BF16)]),
        compiler_params=params(("arbitrary",)),
        cost_estimate=cost(2 * rows * dim * (width + 2 * HEAD), 60e6),
        name="hid_bwd",
    )(meta, dq, dk_part, dv_part, dkv_theirs, k_raw, cos_t, sin_t, kg1, wq, wk, wv, x, pre1, dy_own, dy_mate, img_flag)


def pick_kernel(meta, mine0, theirs0, mine1, theirs1, out_ref, blk):
    n = pl.program_id(0)
    off = meta[2, n]
    for slot, mine, theirs in ((0, mine0, theirs0), (1, mine1, theirs1)):
        is_mine = meta[3 + slot, n] == 1

        @pl.when(is_mine)
        def _():
            blk[...] = mine[...]

        @pl.when(jnp.logical_not(is_mine))
        def _():
            blk[...] = theirs[...]

        src = iota((BLOCK, RB), 0) + off - slot * RB
        pick = (src == iota((BLOCK, RB), 1)).astype(BF16)
        if slot == 0:
            out_ref[...] = dot(pick, blk[...]).astype(BF16)
        else:
            out_ref[...] = jnp.where(src[:, :1] >= 0, dot(pick, blk[...]).astype(BF16), out_ref[...])


def pick_call(meta, mine, theirs):
    dim = mine.shape[1]
    n_img = meta.shape[1]
    at = lambda slot: pl.BlockSpec((RB, dim), lambda n, meta: (meta[slot, n], 0))
    return pl.pallas_call(
        pick_kernel,
        out_shape=jax.ShapeDtypeStruct((n_img * BLOCK, dim), BF16),
        grid_spec=pltpu.PrefetchScalarGridSpec(
            num_scalar_prefetch=1, grid=(n_img,),
            in_specs=[at(0), at(0), at(1), at(1)],
            out_specs=pl.BlockSpec((BLOCK, dim), lambda n, meta: (n, 0)),
            scratch_shapes=[pltpu.VMEM((RB, dim), BF16)]),
        compiler_params=params(("arbitrary",)),
        cost_estimate=cost(4 * n_img * BLOCK * RB * dim, 20e6),
        name="pick_rows",
    )(meta, mine, theirs, mine, theirs)


def gain_norm(values, gain_vec):
    wide = values.astype(F32)
    return (wide * lax.rsqrt(jnp.mean(wide * wide, axis=-1, keepdims=True) + EPS) * (1.0 + gain_vec)).astype(BF16)


def tdot(a, b):
    return lax.dot_general(a, b, (((0,), (0,)), ((), ())), preferred_element_type=F32)


def solution(mesh):
    n_dev = mesh.shape['cp']
    seq_spec = P(('dp', 'cp'))
    part_spec = P('dp')
    rep_spec = P()
    across = [(i, n_dev - 1 - i) for i in range(n_dev)]
    beside = [(i, i ^ 1) for i in range(n_dev)]

    def swap_x(v):
        return lax.ppermute(v, 'cp', across)

    def swap_c(v):
        return lax.ppermute(v, 'cp', beside)

    def device_body(vis_loc, text_loc, img_pos, grad_y, pn_gain, w_proj, pre_gain, w_query, w_key, w_value, q_gain, k_gain, w_out, post_gain):
        dev = lax.axis_index('cp')
        seq_loc, dim = text_loc.shape
        seq = seq_loc * n_dev
        mate = n_dev - 1 - dev
        lo_dev, hi_dev = jnp.minimum(dev, mate), jnp.maximum(dev, mate)
        is_lo = dev < mate
        my_set = lo_dev
        first = my_set == 0
        pre1 = (1.0 + pre_gain.astype(F32))[None]
        post1 = (1.0 + post_gain.astype(F32))[None]
        qg1 = (1.0 + q_gain.astype(F32))[None]
        kg1 = (1.0 + k_gain.astype(F32))[None]

        blocks = 2 * seq_loc // RB
        half = blocks // 2
        blk = jnp.arange(blocks)
        blk_base = jnp.where(blk < half, lo_dev * seq_loc + blk * RB, hi_dev * seq_loc + (blk - half) * RB)
        row = jnp.arange(2 * seq_loc)
        pos = jnp.where(row < seq_loc, lo_dev * seq_loc + row, (hi_dev - 1) * seq_loc + row)
        img = jnp.arange(img_pos.shape[0])
        img_dev = img // 2
        img_set = jnp.minimum(img_dev, n_dev - 1 - img_dev)
        img_slot = jnp.where(img_set == my_set, 0, 4) + jnp.where(img_dev >= n_dev // 2, 2, 0) + img % 2
        rel = img_pos[None, :] - blk_base[:, None]
        hit0 = (rel > -BLOCK) & (rel <= 0)
        hit1 = (rel > 0) & (rel < RB)
        pick_of = lambda hit: jnp.sum(jnp.where(hit, img_slot[None], 0), axis=1)
        off_of = lambda hit: jnp.where(jnp.any(hit, axis=1), jnp.sum(jnp.where(hit, rel, 0), axis=1), seq)
        meta = jnp.stack([jnp.where(is_lo, 1, 0) + 0 * blk, pick_of(hit0), pick_of(hit1), off_of(hit0), off_of(hit1),
                          blk_base // RB]).astype(jnp.int32)
        offset = pos[:, None] - img_pos[None, :]
        in_blk = (offset >= 0) & (offset < BLOCK)
        lim = jnp.maximum(pos + 1, jnp.max(jnp.where(in_blk, img_pos[None, :] + BLOCK, 0), axis=1)).astype(jnp.int32)
        is_img = jnp.any(in_blk, axis=1).astype(jnp.int32)
        q_base = pos[::BQ]
        span = jnp.stack([q_base // BK, q_base // BM, (jnp.max(lim.reshape(-1, BQ), axis=1) + BM - 1) // BM]).astype(jnp.int32)
        lim_w = jnp.broadcast_to(lim[:, None], (2 * seq_loc, 128))
        flag_w = jnp.broadcast_to(is_img[:, None], (2 * seq_loc, 128))
        inv_freq = ROPE_BASE ** (-jnp.arange(0, HEAD, 2).astype(F32) / HEAD)
        angle = (pos.astype(F32) / ROPE_SCALE)[:, None] * inv_freq[None, :]
        cos_t, sin_t = jnp.cos(angle), jnp.sin(angle)

        pooled_own = pool_patches(vis_loc)
        pooled_mate = swap_x(pooled_own)
        text_src, _ = lax.optimization_barrier((text_loc, pooled_mate))
        text_mate = swap_x(text_src)
        dy_src, _ = lax.optimization_barrier((grad_y, text_mate))
        dy_mate = swap_x(dy_src)
        n_own = pooled_own.shape[0]
        pooled = jnp.where(is_lo, jnp.concatenate([pooled_own, pooled_mate]), jnp.concatenate([pooled_mate, pooled_own]))
        normed, norm_pull = jax.vjp(gain_norm, pooled, pn_gain.astype(F32))
        soft = dot(normed, w_proj).astype(BF16)
        soft_all = jnp.concatenate([soft, swap_c(soft)])

        x, hidden, q_raw, q, k_raw, k, v = qkv_call(meta, text_loc, text_mate, soft_all, pre1, w_query, w_key, w_value, qg1, kg1, cos_t, sin_t)

        def by_position(mine, theirs):
            a = jnp.where(first, mine, theirs)
            b = jnp.where(first, theirs, mine)
            return jnp.concatenate([a[:seq_loc], b, a[seq_loc:]])

        kv = jnp.concatenate([k, v], axis=1)
        kv_all = by_position(kv, swap_c(kv))
        k_all, v_all = kv_all[:, :HEAD], kv_all[:, HEAD:]
        kt_all = k_all.T
        hidden_c = swap_c(hidden)
        o, lse = fwd_call(span, q, kt_all, v_all, lim_w)
        y_loc, d_a, d_o, delta, g_post = out_call(meta, o, x, grad_y, dy_mate, w_out, post1)
        cols = w_query.shape[1] // 2
        pick_cols = lambda v, flag: jnp.where(flag, v[:, :cols], v[:, cols:])
        o_c = swap_c(pick_cols(o, ~first))
        d_a_c = swap_c(d_a)
        delta_t = delta.T[:, None, :]
        dq_raw, g_qg, dk_part, dv_part = bwd_call(span, q, d_o, k_all, kt_all, v_all, lim[None], lse, delta_t, q_raw, qg1, cos_t, sin_t)
        g_out_half = (tdot(pick_cols(o, first), d_a) + tdot(o_c, d_a_c)).astype(BF16)
        g_out_other = swap_c(g_out_half)
        g_out = jnp.where(first, jnp.concatenate([g_out_half, g_out_other]), jnp.concatenate([g_out_other, g_out_half]))

        dkv_part = jnp.concatenate([dk_part, dv_part], axis=1)
        set_a = jnp.concatenate([dkv_part[:seq_loc], dkv_part[3 * seq_loc:]])
        set_b = dkv_part[seq_loc:3 * seq_loc]
        dkv_c = swap_c(jnp.where(first, set_b, set_a))
        grad_text, d_merged, dk_raw, d_v, g_pre, g_kg = hid_call(
            meta, dq_raw, dk_part, dv_part, dkv_c, k_raw, cos_t, sin_t, kg1, w_query, w_key, w_value, x, pre1, grad_y, dy_mate, flag_w)

        d_merged_c = swap_c(d_merged)
        my_img = jnp.concatenate([2 * lo_dev + jnp.arange(2), 2 * hi_dev + jnp.arange(2)])
        start = img_pos[my_img]
        blk0 = start // RB
        blk1 = jnp.minimum(blk0 + 1, seq // RB - 1)

        def locate(g):
            owner = g // half
            in_set = jnp.minimum(owner, n_dev - 1 - owner)
            return g % half + jnp.where(owner >= n_dev // 2, half, 0), (in_set == my_set).astype(jnp.int32)

        at0, mine0 = locate(blk0)
        at1, mine1 = locate(blk1)
        d_soft = pick_call(jnp.stack([at0, at1, start % RB, mine0, mine1]).astype(jnp.int32), d_merged, d_merged_c)
        d_normed = dot_t(d_soft, w_proj).astype(BF16)
        d_pooled, g_pn = norm_pull(d_normed)
        d_own = jnp.where(is_lo, d_pooled[:n_own], d_pooled[n_own:])
        grad_vis = unpool_grad(d_own, vis_loc.shape[0])
        g_proj_part = tdot(normed, d_soft)
        pc = g_proj_part.shape[0] // 2
        p_lo, p_hi = g_proj_part[:pc], g_proj_part[pc:]
        g_proj_half = (jnp.where(first, p_lo, p_hi) + swap_c(jnp.where(first, p_hi, p_lo))).astype(BF16)
        g_proj_other = swap_c(g_proj_half)
        g_proj = jnp.where(first, jnp.concatenate([g_proj_half, g_proj_other]), jnp.concatenate([g_proj_other, g_proj_half]))

        mine = jnp.concatenate([pick_cols(dq_raw, first), jnp.where(first, dk_raw, d_v)], axis=1)
        dq_c = swap_c(pick_cols(dq_raw, ~first))
        kv_c = swap_c(jnp.where(first, d_v, dk_raw))
        theirs = jnp.concatenate([dq_c, kv_c], axis=1)
        g_half = (tdot(hidden, mine) + tdot(hidden_c, theirs)).astype(BF16)
        g_other = swap_c(g_half)
        g_a = jnp.where(first, g_half, g_other)
        g_b = jnp.where(first, g_other, g_half)
        g_query = jnp.concatenate([g_a[:, :cols], g_b[:, :cols]], axis=1)
        g_key, g_value = g_a[:, cols:], g_b[:, cols:]

        small = jnp.concatenate([g_pn, g_pre[0], g_qg[0], g_kg[0], g_post[0]])
        small = (small + swap_c(small)).astype(BF16)
        cuts = [g_pn.shape[0]]
        for g in (g_pre, g_qg, g_kg):
            cuts.append(cuts[-1] + g.shape[1])
        g_pn, g_pre, g_qg, g_kg, g_post = jnp.split(small, cuts)
        return (y_loc, grad_text, grad_vis, g_pn, g_proj, g_pre, g_query, g_key, g_value, g_qg, g_kg, g_out, g_post)

    in_specs = (seq_spec, seq_spec, part_spec, seq_spec) + (rep_spec,) * 10
    out_specs = (seq_spec, seq_spec, seq_spec) + (part_spec,) * 10
    return jax.shard_map(device_body, mesh=mesh, in_specs=in_specs, out_specs=out_specs, check_vma=False)
```

time: 1900 us -> 839 us (0.44)
  blocking collectives: 795 us -> 0 us
  Pallas kernels: 0 us -> 487 us
  matrix products: 397 us -> 95.4 us
  other arithmetic: 347 us -> 84.5 us
  local copies, waits for them, and re-layouts: 241 us -> 49.4 us
    psum x1 -> x0, blocking collectives: 795 us -> none  [device_body(): lax.psum((g_pn, g_proj, g_pre, g_query, g_key, g_value, g_q_gain, g_k_gai...]
    pallas_call x0 -> x8, Pallas kernels: none -> 487 us  [the longest x1 175 us: bwd_call(): pl.pallas_call(bwd_kernel, out_shape=[jax.ShapeDtypeStruct((rows, width),...]
    dot_general x21 -> x7, matrix products: 397 us -> 95.4 us  [the longest x5 72.6 us: tdot(): lax.dot_general(a, b, (((0,), (0,)), ((), ())), preferred_element_type=F32)]
    another operation x2, other arithmetic: 172 us -> 0.6 us  [device_body(): jnp.stack([q_base // BK, q_base // BM, (jnp.max(lim.reshape(-1, BQ), axis...]
    ppermute x0 -> x17, waiting for transfers between devices: none -> 100 us  [the longest x3 100 us: swap_x(): return lax.ppermute(v, 'cp', across)]
    reduce_sum x9 -> x2, other arithmetic: 91.7 us -> 3.14 us  [the longest x1 2.92 us: gain_norm(): jnp.mean(wide * wide, axis=-1, keepdims=True) + EPS]
    another operation x1 -> x3, local copies, waits for them, and re-layouts: 87.3 us -> 1.23 us  [the longest x2 0.62 us: device_body(): jnp.stack([jnp.where(is_lo, 1, 0) + 0 * blk, pick_of(hit0), pick_of(hit1)...]
    all_gather x3 -> x0, waiting for transfers between devices: 50.5 us -> none  [the longest x1 50.5 us: device_body(): soft_all = lax.all_gather(soft_loc, 'cp', tiled=True)]
  transfers between devices with their start and end apart: 6 -> 17, of which waited for: 2 -> 2; matrix products, arithmetic and copies ran while one was open for 27% -> 25% of each run, Pallas kernels for 0% -> 52%
where the time goes in v1:
time: 839 us; the launch traced here: 829 us
  Pallas kernels  487 us (58%)
  waiting for transfers between devices  100 us (12%)
  matrix products  95.4 us (11%)
  other arithmetic  84.5 us (10%)
  local copies, waits for them, and re-layouts  49.4 us (6%)
  starting transfers between devices  11.5 us (1%)
    pallas_call x1, Pallas kernels, bwd_call(): pl.pallas_call(bwd_kernel, out_shape=[jax.ShapeDtypeStruct((rows, width),...  175 us
    pallas_call x1, Pallas kernels, fwd_call(): pl.pallas_call(fwd_kernel, out_shape=[jax.ShapeDtypeStruct((rows, width),...  142 us
    ppermute x3, waiting for transfers between devices, swap_x(): return lax.ppermute(v, 'cp', across)  100 us
    dot_general x5, matrix products, tdot(): lax.dot_general(a, b, (((0,), (0,)), ((), ())), preferred_element_type=F32)  72.6 us
    pallas_call x1, Pallas kernels, out_call(): pl.pallas_call(out_kernel, out_shape=[jax.ShapeDtypeStruct(dy_own.shape,...  54.1 us
    pallas_call x1, Pallas kernels, hid_call(): pl.pallas_call(hid_kernel, out_shape=[jax.ShapeDtypeStruct(dy_own.shape,...  43.3 us
    pallas_call x1, Pallas kernels, qkv_call(): pl.pallas_call(qkv_kernel, out_shape=[struct(dim), struct(dim), struct(wi...  40.9 us
    unnamed x67, local copies, waits for them, and re-layouts  22.9 us
  transfers between devices with their start and end apart: 17, of which 2 were waited for; matrix products, arithmetic and copies ran while one was open for 25% of the time, Pallas kernels for 52%

profile of v1, /device:TPU:0, one launch (start us, length us, event | category | flops | bytes accessed | tf_op | source)
XLA Modules:
  0.0 829.4 jit_solution(6193751836398599599)
XLA Ops:
  0.7 10.4 %pool.1 = bf16[512,1152]{1,0:T(8,128)(2,1)} custom-call(bf16[2,4096,1152]{2,1,0:T(8,128)(2,1)} %vis_ref.1), custom_call_target="tpu_custom_call" | custom-call | flops 4000000000 | bytes 18874368 | tf_op jit(solution)/shard_map/pool/pallas_call | solution.py:65
  11.1 2.8 collective-permute-start
  13.9 26.3 %collective-permute-done = bf16[512,1152]{1,0:T(8,128)(2,1)S(1)} collective-permute-done((bf16[512,1152]{1,0:T(8,128)(2,1)}, bf16[512,1152]{1,0:T(8,128)(2,1)S(1)}, u32[]{:S(2)}, u32[]{:S(2)}) %collective-permute-start) | collective-permute-done | bytes 1179680 | tf_op jit(solution)/shard_map/ppermute | solution.py:528
  40.2 2.9 fusion.12
  43.8 12.0 %convolution_convert_fusion.1 = bf16[1024,2048]{1,0:T(8,128)(2,1)} fusion(bf16[1152,2048]{1,0:T(8,128)(2,1)} %param.19, f32[1152]{0:T(1024)S(1)} %convert_add_fusion.2, f32[1024]{0:T(1024)S(1)} %fusion.33, bf16[512,1152]{1,0:T(8,128)(2,1)S(1)} %collective-permute-done, bf16[512,1152]{1,0:T(8,128)(2,1)} %pool.1, pred[]{:T(512)S(6)} %lt.93), kind=kOutput, calls=%fused_computation.41 | convolution fusion | flops 4849270784 | bytes 11280897 | tf_op jit(solution)/shard_map/dot_general | solution.py:37
  55.9 2.5 collective-permute-start.1
  58.9 0.6 stack.36.meta
  60.7 0.6 convert_add_fusion.1
  61.3 5.5 multiply_sine_fusion
  66.8 8.5 %pad_maximum_fusion.soft_a.soft_b = bf16[2048,2048]{1,0:T(8,128)(2,1)} fusion(bf16[1024,2048]{1,0:T(8,128)(2,1)} %collective-permute-done.2, bf16[1024,2048]{1,0:T(8,128)(2,1)} %convolution_convert_fusion.1), kind=kLoop, calls=%fused_computation.2 | loop fusion | flops 16777216 | bytes 16777216 | tf_op jit(solution)/shard_map/concatenate | solution.py:586
  75.3 73.9 %collective-permute-done.1.text_mate = bf16[1024,2048]{1,0:T(8,128)(2,1)} collective-permute-done((bf16[1024,2048]{1,0:T(8,128)(2,1)}, bf16[1024,2048]{1,0:T(8,128)(2,1)}, u32[]{:S(2)}, u32[]{:S(2)}) %collective-permute-start.1) | collective-permute-done | bytes 4194336 | tf_op jit(solution)/shard_map/ppermute | solution.py:528
  149.2 40.9 %qkv.1 = (bf16[2048,2048]{1,0:T(8,128)(2,1)}, bf16[2048,2048]{1,0:T(8,128)(2,1)}, bf16[2048,2048]{1,0:T(8,128)(2,1)}, bf16[2048,2048]{1,0:T(8,128)(2,1)}, bf16[2...) custom-call(s32[6,8]{1,0:T(8,128)} %stack.36.meta, bf16[1024,2048]{1,0:T(8,128)(2,1)} %text_own.1, ...), custom_call_target="tpu_custom_call" | custom-call | flops 21474836480 | bytes 60000000 | tf_op jit(solution)/shard_map/qkv/pallas_call | solution.py:190
  190.1 1.3 constant_dynamic-update-slice_fusion.1
  191.4 1.3 constant_dynamic-update-slice_fusion
  192.7 1.2 collective-permute-start.3
  194.4 0.6 pad_add_fusion.span
  195.0 0.6 convert_add_fusion
  195.6 0.6 fusion.27.lim_ref
  196.2 1.7 collective-permute-start.4
  197.9 2.1 broadcast_select_fusion.5
  200.6 2.5 fusion.46
  203.1 2.9 copy.39.kt_ref
  206.0 1.3 broadcast_in_dim.93.lim_ref
  207.3 142.3 %attn_fwd.1 = (bf16[2048,2048]{1,0:T(8,128)(2,1)}, f32[8,1,2048]{2,1,0:T(1,128)}) custom-call(s32[3,4]{1,0:T(4,128)} %pad_add_fusion.span, bf16[2048,2048]{1,0:T(8,128)(2,1)} %get-tuple-element.40.q_ref, bf16[256,4096]{1,0:T(8,128)(2,1)} %copy.39.kt_ref, bf16[4096,256]{1,0:T(8,128)(2,1)} %get-tuple-element.122.v_ref, s32[2048,128]{1,0:T(8,128)} %broadcast_in_dim.93.lim_ref), custom_call_target="tpu_custom_call" | custom-call | flops 34359738368 | bytes 30000000 | tf_op jit(solution)/shard_map/attn_fwd/pallas_call | solution.py:245
  349.6 54.1 %out_proj.1 = (bf16[1024,2048]{1,0:T(8,128)(2,1)}, bf16[2048,2048]{1,0:T(8,128)(2,1)}, bf16[2048,2048]{1,0:T(8,128)(2,1)}, f32[2048,8]{1,0:T(8,128)}, f32[1,2048]{1,0:T(1,128)}) custom-call(s32[6,8]{1,0:T(8,128)} %stack.36.meta, bf16[2048,2048]{1,0:T(8,128)(2,1)} %get-tuple-element.43.o_ref, bf16[2048,2048]{1,0:T(8,128)(2,1)} %get-tuple-element.44.x_ref, ...), custom_call_target="tpu_custom_call" | custom-call | flops 34359738368 | bytes 60000000 | tf_op jit(solution)/shard_map/out_proj/pallas_call | solution.py:385
  403.7 1.5 copy.40
  405.3 0.7 broadcast_in_dim.95.delta_ref
  405.9 174.5 %attn_bwd.1 = (bf16[2048,2048]{1,0:T(8,128)(2,1)}, f32[1,256]{1,0:T(1,128)}, f32[4096,256]{1,0:T(8,128)}, f32[4096,256]{1,0:T(8,128)}) custom-call(s32[3,4]{1,0:T(4,128)} %pad_add_fusion.span, bf16[2048,2048]{1,0:T(8,128)(2,1)} %get-tuple-element.40.q_ref, bf16[2048,2048]{1,0:T(8,128)(2,1)} %get-tuple-element.47.do_ref, ...), custom_call_target="tpu_custom_call" | custom-call | flops 85899345920 | bytes 50000000 | tf_op jit(solution)/shard_map/attn_bwd/pallas_call | solution.py:312
  580.5 3.0 constant_dynamic-update-slice_fusion.3
  583.9 1.1 constant_dynamic-update-slice_fusion.2
  585.5 3.0 slice_select_fusion.1
  589.0 5.9 broadcast_select_fusion.4
  595.6 0.6 gather_fusion
  596.3 1.4 broadcast_in_dim.96.lim_ref
  597.7 43.3 %hid_bwd.1 = (bf16[1024,2048]{1,0:T(8,128)(2,1)}, bf16[2048,2048]{1,0:T(8,128)(2,1)}, bf16[2048,256]{1,0:T(8,128)(2,1)}, bf16[2048,256]{1,0:T(8,128)(2,1)}, f32[1,2048]{1,0:T(1,128)}, /*index=5*/f32[1,256]{1,0:T(1,128)}) custom-call(s32[6,8]{1,0:T(8,128)} %stack.36.meta, bf16[2048,2048]{1,0:T(8,128)(2,1)} %get-tuple-element.51.dq_ref, ...), custom_call_target="tpu_custom_call" | custom-call | flops 21474836480 | bytes 60000000 | tf_op jit(solution)/shard_map/hid_bwd/pallas_call | solution.py:451
  640.9 1.7 broadcast_select_fusion.8
  642.7 0.6 stack.40.meta
  643.3 3.7 broadcast_select_fusion.2
  647.6 18.4 %fusion.5 = f32[2048,1280]{0,1:T(8,128)} fusion(bf16[2048,2048]{1,0:T(8,128)(2,1)} %collective-permute-done.10, bf16[2048,256]{1,0:T(8,128)(2,1)} %collective-permute-done.12, bf16[2048,1024]{1,0:T(8,128)(2,1)} %collective-permute-done.11), kind=kOutput, calls=%fused_computation.18 | convolution fusion | flops 10747904000 | bytes 24117248 | tf_op jit(solution)/shard_map/dot_general | solution.py:516
  666.0 17.9 %add_convert_fusion = bf16[2048,1280]{0,1:T(8,128)(2,1)} fusion(f32[2048,1280]{0,1:T(8,128)} %fusion.5, bf16[2048,2048]{1,0:T(8,128)(2,1)} %get-tuple-element.61, bf16[2048,256]{1,0:T(8,128)(2,1)S(1)} %get-tuple-element.125, bf16[2048,1024]{1,0:T(8,128)(2,1)} %get-tuple-element.116), kind=kOutput, calls=%fused_computation.1 | convolution fusion | flops 10753146880 | bytes 29360128 | tf_op jit(solution)/shard_map/dot_general | solution.py:516
  684.4 13.1 %fusion.50 = f32[1024,2048]{1,0:T(8,128)S(1)} fusion(bf16[2048,1024]{1,0:T(8,128)(2,1)} %collective-permute-done.14, bf16[2048,2048]{1,0:T(8,128)(2,1)} %collective-permute-done.15), kind=kOutput, calls=%fused_computation.173 | convolution fusion | flops 8589934592 | bytes 20971520 | tf_op jit(solution)/shard_map/dot_general | solution.py:516
  697.5 15.6 %add_convert_fusion.1 = bf16[1024,2048]{1,0:T(8,128)(2,1)} fusion(f32[1024,2048]{1,0:T(8,128)S(1)} %fusion.50, bf16[2048,2048]{1,0:T(8,128)(2,1)} %get-tuple-element.64, pred[]{:T(512)S(6)} %eq.45, bf16[2048,2048]{1,0:T(8,128)(2,1)} %get-tuple-element.43.o_ref), kind=kOutput, calls=%fused_computation.5 | convolution fusion | flops 8596226048 | bytes 29360128 | tf_op jit(solution)/shard_map/dot_general | solution.py:516
  713.2 10.6 %pick_rows.1 = bf16[1024,2048]{1,0:T(8,128)(2,1)} custom-call(s32[5,4]{1,0:T(8,128)} %stack.40.meta, bf16[2048,2048]{1,0:T(8,128)(2,1)} %get-tuple-element.56.mine0.mine1, bf16[2048,2048]{1,0:T(8,128)(2,1)} %collective-permute-done.6.theirs0.theirs1, bf16[2048,2048]{1,0:T(8,128)(2,1)} %get-tuple-element.56.mine0.mine1, ...), custom_call_target="tpu_custom_call" | custom-call | flops 2147483648 | bytes 20000000 | tf_op jit(solution)/shard_map/pick_rows/pallas_call | solution.py:496
  723.8 7.6 fusion.21
  731.4 3.6 slice_select_fusion
  735.0 1.5 copy-done.2
  737.0 8.8 %broadcast_select_fusion.1 = (bf16[2048,1280]{0,1:T(8,128)(2,1)}, bf16[2048,1280]{0,1:T(8,128)(2,1)}) fusion(bf16[2048,1280]{0,1:T(8,128)(2,1)} %add_convert_fusion, bf16[2048,1280]{0,1:T(8,128)(2,1)} %collective-permute-done.13, pred[]{:T(512)S(6)} %eq.45), kind=kLoop, calls=%fused_computation.23 | loop fusion | flops 5242880 | bytes 20971520 | tf_op jit(solution)/shard_map/jit(_where)/select_n | solution.py:650
  745.9 4.9 slice.97
  750.7 1.3 slice.99
  752.1 2.3 slice.98
  754.4 1.1 slice.100
  755.5 8.5 %pad_maximum_fusion.1 = bf16[2048,2048]{0,1:T(8,128)(2,1)} fusion(bf16[2048,1024]{0,1:T(8,128)(2,1)} %slice.98, bf16[2048,1024]{0,1:T(8,128)(2,1)} %slice.97), kind=kLoop, calls=%fused_computation.3 | loop fusion | flops 16777216 | bytes 16777216 | tf_op jit(solution)/shard_map/concatenate | solution.py:652
  764.0 12.2 %copy.42 = bf16[2048,2048]{1,0:T(8,128)(2,1)} copy(bf16[2048,2048]{0,1:T(8,128)(2,1)} %pad_maximum_fusion.1) | data formatting | bytes 16777216
  776.2 1.3 copy.43
  777.5 2.3 copy.44
  779.9 10.8 %fusion.10 = (f32[1152]{0:T(1024)S(1)}, f32[1024]{0:T(1024)S(1)}, bf16[1024,1152]{1,0:T(8,128)(2,1)S(1)}) fusion(f32[1024]{0:T(1024)S(1)} %copy-done.14, bf16[512,1152]{1,0:T(8,128)(2,1)S(1)} %copy-done.3, bf16[512,1152]{1,0:T(8,128)(2,1)S(1)} %copy-done.5, pred[]{:T(512)S(6)} %lt.93, f32[1152]{0:T(1024)S(1)} %copy-done.12, ...), kind=kOutput, calls=%fused_computation.25 | convolution fusion | flops 4853069824 | bytes 13648897 | tf_op jit(solution)/shard_map/dot_general | solution.py:41
  791.0 4.7 fusion.11
  795.8 3.6 add_convert_fusion.2
  799.8 1.1 slice_select_fusion.2.d_ref
  800.9 10.6 %unpool.1 = bf16[2,4096,1152]{2,1,0:T(8,128)(2,1)} custom-call(bf16[512,1152]{1,0:T(8,128)(2,1)} %slice_select_fusion.2.d_ref), custom_call_target="tpu_custom_call" | custom-call | flops 4000000000 | bytes 18874368 | tf_op jit(solution)/shard_map/unpool/pallas_call | solution.py:90
  811.6 10.2 %maximum_select_fusion = bf16[2048,2048]{1,0:T(8,128)(2,1)} fusion(bf16[1024,2048]{1,0:T(8,128)(2,1)} %collective-permute-done.16, bf16[1024,2048]{1,0:T(8,128)(2,1)} %add_convert_fusion.1, pred[]{:T(512)S(6)} %eq.45), kind=kLoop, calls=%fused_computation.4 | loop fusion | flops 37748736 | bytes 16777216 | tf_op jit(solution)/shard_map/jit(_where)/select_n | solution.py:610
  821.7 0.6 split.20
  822.8 0.6 fusion.48
  823.5 5.5 maximum_select_fusion.1
  (129 shorter events, 8.4 us)
Async XLA Ops:
  0.6 13.2 %copy-start.17 = (bf16[1152]{0:T(1024)(128)(2,1)S(1)}, bf16[1152]{0:T(1024)(128)(2,1)}, u32[]{:S(2)}) copy-start(bf16[1152]{0:T(1024)(128)(2,1)} %param.18) | copy-start | bytes 6916
  11.1 29.1 %collective-permute-start = (bf16[512,1152]{1,0:T(8,128)(2,1)}, bf16[512,1152]{1,0:T(8,128)(2,1)S(1)}, u32[]{:S(2)}, u32[]{:S(2)}) collective-permute-start(bf16[512,1152]{1,0:T(8,128)(2,1)} %pool.1), channel_id=1, source_target_pairs={{0,3},{1,2},{2,1},{3,0},{4,7},{5,6},{6,5},{7,4}} | collective-permute-start | bytes 3538952 | tf_op jit(solution)/shard_map/ppermute | solution.py:528
  13.9 41.9 %copy-start.11 = (f32[1152]{0:T(1024)}, f32[1152]{0:T(1024)S(1)}, u32[]{:S(2)}) copy-start(f32[1152]{0:T(1024)S(1)} %convert_add_fusion.2) | copy-start | bytes 13828
  40.2 15.5 %copy-start.4 = (bf16[512,1152]{1,0:T(8,128)(2,1)}, bf16[512,1152]{1,0:T(8,128)(2,1)S(1)}, u32[]{:S(2)}) copy-start(bf16[512,1152]{1,0:T(8,128)(2,1)S(1)} %collective-permute-done) | copy-start | bytes 3538948
  43.1 0.6 copy-start.9
  43.7 12.0 %copy-start.13 = (f32[1024]{0:T(1024)}, f32[1024]{0:T(1024)S(1)}, u32[]{:S(2)}) copy-start(f32[1024]{0:T(1024)S(1)} %fusion.33) | copy-start | bytes 12292
  43.7 14.7 %copy-start = (s32[8]{0:T(128)S(1)}, s32[8]{0:T(128)}, u32[]{:S(2)}) copy-start(s32[8]{0:T(128)} %param.16) | copy-start | bytes 100
  43.7 15.7 %copy-start.22 = (bf16[256]{0:T(256)(128)(2,1)S(1)}, bf16[256]{0:T(256)(128)(2,1)}, u32[]{:S(2)}) copy-start(bf16[256]{0:T(256)(128)(2,1)} %param.24) | copy-start | bytes 1540
  43.7 16.3 %copy-start.23 = (bf16[256]{0:T(256)(128)(2,1)S(1)}, bf16[256]{0:T(256)(128)(2,1)}, u32[]{:S(2)}) copy-start(bf16[256]{0:T(256)(128)(2,1)} %param.25) | copy-start | bytes 1540
  43.8 16.9 %copy-start.18 = (bf16[2048]{0:T(1024)(128)(2,1)S(1)}, bf16[2048]{0:T(1024)(128)(2,1)}, u32[]{:S(2)}) copy-start(bf16[2048]{0:T(1024)(128)(2,1)} %param.20) | copy-start | bytes 12292
  55.8 11.0 %collective-permute-start.2 = (bf16[1024,2048]{1,0:T(8,128)(2,1)}, bf16[1024,2048]{1,0:T(8,128)(2,1)}, u32[]{:S(2)}, u32[]{:S(2)}) collective-permute-start(bf16[1024,2048]{1,0:T(8,128)(2,1)} %convolution_convert_fusion.1), channel_id=1, source_target_pairs={{0,1},{1,0},{2,3},{3,2},{4,5},{5,4},{6,7},{7,6}} | collective-permute-start | bytes 12582920 | tf_op jit(solution)/shard_map/ppermute | solution.py:531
  55.9 93.3 %collective-permute-start.1 = (bf16[1024,2048]{1,0:T(8,128)(2,1)}, bf16[1024,2048]{1,0:T(8,128)(2,1)}, u32[]{:S(2)}, u32[]{:S(2)}) collective-permute-start(bf16[1024,2048]{1,0:T(8,128)(2,1)} %text_own.1), channel_id=1, source_target_pairs={{0,3},{1,2},{2,1},{3,0},{4,7},{5,6},{6,5},{7,4}} | collective-permute-start | bytes 12582920 | tf_op jit(solution)/shard_map/ppermute | solution.py:528
  149.2 45.7 %copy-start.19 = (bf16[2048]{0:T(1024)(128)(2,1)S(1)}, bf16[2048]{0:T(1024)(128)(2,1)}, u32[]{:S(2)}) copy-start(bf16[2048]{0:T(1024)(128)(2,1)} %param.27) | copy-start | bytes 12292
  192.7 5.1 collective-permute-start.3
  194.0 6.2 copy-start.7
  196.2 153.5 %collective-permute-start.4 = (bf16[1024,2048]{1,0:T(8,128)(2,1)}, bf16[1024,2048]{1,0:T(8,128)(2,1)}, u32[]{:S(2)}, u32[]{:S(2)}) collective-permute-start(bf16[1024,2048]{1,0:T(8,128)(2,1)} %dy_own.3), channel_id=1, source_target_pairs={{0,3},{1,2},{2,1},{3,0},{4,7},{5,6},{6,5},{7,4}} | collective-permute-start | bytes 12582920 | tf_op jit(solution)/shard_map/ppermute | solution.py:528
  197.8 449.7 %collective-permute-start.10 = (bf16[2048,2048]{1,0:T(8,128)(2,1)}, bf16[2048,2048]{1,0:T(8,128)(2,1)}, u32[]{:S(2)}, u32[]{:S(2)}) collective-permute-start(bf16[2048,2048]{1,0:T(8,128)(2,1)} %get-tuple-element.61), channel_id=1, source_target_pairs={{0,1},{1,0},{2,3},{3,2},{4,5},{5,4},{6,7},{7,6}} | collective-permute-start | bytes 25165832 | tf_op jit(solution)/shard_map/ppermute | solution.py:531
  580.5 3.5 copy-start.6
  588.5 7.7 collective-permute-start.5
  589.0 5.9 copy-start.1
  589.0 5.9 copy-start.8
  594.9 52.7 %collective-permute-start.11 = (bf16[2048,1024]{1,0:T(8,128)(2,1)}, bf16[2048,1024]{1,0:T(8,128)(2,1)}, u32[]{:S(2)}, u32[]{:S(2)}) collective-permute-start(bf16[2048,1024]{1,0:T(8,128)(2,1)} %get-tuple-element.117), channel_id=1, source_target_pairs={{0,1},{1,0},{2,3},{3,2},{4,5},{5,4},{6,7},{7,6}} | collective-permute-start | bytes 12582920 | tf_op jit(solution)/shard_map/ppermute | solution.py:531
  595.0 89.3 %collective-permute-start.15 = (bf16[2048,2048]{1,0:T(8,128)(2,1)}, bf16[2048,2048]{1,0:T(8,128)(2,1)}, u32[]{:S(2)}, u32[]{:S(2)}) collective-permute-start(bf16[2048,2048]{1,0:T(8,128)(2,1)} %get-tuple-element.64), channel_id=1, source_target_pairs={{0,1},{1,0},{2,3},{3,2},{4,5},{5,4},{6,7},{7,6}} | collective-permute-start | bytes 25165832 | tf_op jit(solution)/shard_map/ppermute | solution.py:531
  642.6 5.0 collective-permute-start.12
  647.0 37.3 %collective-permute-start.14 = (bf16[2048,1024]{1,0:T(8,128)(2,1)S(1)}, bf16[2048,1024]{1,0:T(8,128)(2,1)}, u32[]{:S(2)}, u32[]{:S(2)}) collective-permute-start(bf16[2048,1024]{1,0:T(8,128)(2,1)S(1)} %broadcast_select_fusion.2), channel_id=1, source_target_pairs={{0,1},{1,0},{2,3},{3,2},{4,5},{5,4},{6,7},{7,6}} | collective-permute-start | bytes 12582920 | tf_op jit(solution)/shard_map/ppermute | solution.py:531
  647.5 65.6 %collective-permute-start.6 = (bf16[2048,2048]{1,0:T(8,128)(2,1)}, bf16[2048,2048]{1,0:T(8,128)(2,1)}, u32[]{:S(2)}, u32[]{:S(2)}) collective-permute-start(bf16[2048,2048]{1,0:T(8,128)(2,1)} %get-tuple-element.56.mine0.mine1), channel_id=1, source_target_pairs={{0,1},{1,0},{2,3},{3,2},{4,5},{5,4},{6,7},{7,6}} | collective-permute-start | bytes 25165832 | tf_op jit(solution)/shard_map/ppermute | solution.py:531
  683.9 53.1 %collective-permute-start.13 = (bf16[2048,1280]{0,1:T(8,128)(2,1)}, bf16[2048,1280]{0,1:T(8,128)(2,1)}, u32[]{:S(2)}, u32[]{:S(2)}) collective-permute-start(bf16[2048,1280]{0,1:T(8,128)(2,1)} %add_convert_fusion), channel_id=1, source_target_pairs={{0,1},{1,0},{2,3},{3,2},{4,5},{5,4},{6,7},{7,6}} | collective-permute-start | bytes 15728648 | tf_op jit(solution)/shard_map/ppermute | solution.py:531
  713.1 10.7 %copy-start.3 = (bf16[512,1152]{1,0:T(8,128)(2,1)S(1)}, bf16[512,1152]{1,0:T(8,128)(2,1)}, u32[]{:S(2)}) copy-start(bf16[512,1152]{1,0:T(8,128)(2,1)} %pool.1) | copy-start | bytes 3538948
  713.1 10.7 %copy-start.5 = (bf16[512,1152]{1,0:T(8,128)(2,1)S(1)}, bf16[512,1152]{1,0:T(8,128)(2,1)}, u32[]{:S(2)}) copy-start(bf16[512,1152]{1,0:T(8,128)(2,1)} %copy-done.4) | copy-start | bytes 3538948
  713.1 10.7 %copy-start.12 = (f32[1152]{0:T(1024)S(1)}, f32[1152]{0:T(1024)}, u32[]{:S(2)}) copy-start(f32[1152]{0:T(1024)} %copy-done.11) | copy-start | bytes 13828
  713.1 10.7 %copy-start.14 = (f32[1024]{0:T(1024)S(1)}, f32[1024]{0:T(1024)}, u32[]{:S(2)}) copy-start(f32[1024]{0:T(1024)} %copy-done.13) | copy-start | bytes 12292
  713.1 98.5 %collective-permute-start.16 = (bf16[1024,2048]{1,0:T(8,128)(2,1)}, bf16[1024,2048]{1,0:T(8,128)(2,1)}, u32[]{:S(2)}, u32[]{:S(2)}) collective-permute-start(bf16[1024,2048]{1,0:T(8,128)(2,1)} %add_convert_fusion.1), channel_id=1, source_target_pairs={{0,1},{1,0},{2,3},{3,2},{4,5},{5,4},{6,7},{7,6}} | collective-permute-start | bytes 12582920 | tf_op jit(solution)/shard_map/ppermute | solution.py:531
  731.4 5.2 copy-start.2
  736.6 59.1 %collective-permute-start.8 = (f32[576,2048]{1,0:T(8,128)}, f32[576,2048]{1,0:T(8,128)}, u32[]{:S(2)}, u32[]{:S(2)}) collective-permute-start(f32[576,2048]{1,0:T(8,128)} %slice_select_fusion), channel_id=1, source_target_pairs={{0,1},{1,0},{2,3},{3,2},{4,5},{5,4},{6,7},{7,6}} | collective-permute-start | bytes 14155784 | tf_op jit(solution)/shard_map/ppermute | solution.py:531
  745.8 6.2 slice-start.3
  745.8 6.2 slice-start.4
  777.5 18.2 %slice-start = ((s8[9437184]{0:T(1024)(128)(4,1)}), s8[1048576]{0:T(1024)(128)(4,1)S(1)}, s32[]{:S(2)}) async-start(s8[9437184]{0:T(1024)(128)(4,1)} %bitcast.80), calls=%async_computation | async-start | bytes 2097152
  779.9 10.9 %copy-start.16 = (f32[1,2048]{1,0:T(1,128)S(1)}, f32[1,2048]{1,0:T(1,128)}, u32[]{:S(2)}) copy-start(f32[1,2048]{1,0:T(1,128)} %get-tuple-element.57) | copy-start | bytes 24580
  779.9 10.9 %copy-start.20 = (f32[1,256]{1,0:T(1,128)S(1)}, f32[1,256]{1,0:T(1,128)}, u32[]{:S(2)}) copy-start(f32[1,256]{1,0:T(1,128)} %get-tuple-element.58) | copy-start | bytes 3076
  779.9 10.9 %copy-start.21 = (f32[1,256]{1,0:T(1,128)S(1)}, f32[1,256]{1,0:T(1,128)}, u32[]{:S(2)}) copy-start(f32[1,256]{1,0:T(1,128)} %get-tuple-element.59) | copy-start | bytes 3076
  779.9 11.0 %copy-start.15 = (f32[1,2048]{1,0:T(1,128)S(1)}, f32[1,2048]{1,0:T(1,128)}, u32[]{:S(2)}) copy-start(f32[1,2048]{1,0:T(1,128)} %get-tuple-element.60) | copy-start | bytes 24580
  779.9 11.1 %copy-start.10 = (f32[1024]{0:T(1024)S(1)}, f32[1024]{0:T(1024)}, u32[]{:S(2)}) copy-start(f32[1024]{0:T(1024)} %copy-done.9) | copy-start | bytes 12292
  779.9 15.8 %slice-start.1 = ((s8[9437184]{0:T(1024)(128)(4,1)}), s8[4194304]{0:T(1024)(128)(4,1)S(1)}, s32[]{:S(2)}) async-start(s8[9437184]{0:T(1024)(128)(4,1)} %bitcast.80), calls=%async_computation.1 | async-start | bytes 8388608
  779.9 15.8 %slice-start.2 = ((s8[9437184]{0:T(1024)(128)(4,1)}), s8[4194304]{0:T(1024)(128)(4,1)S(1)}, s32[]{:S(2)}) async-start(s8[9437184]{0:T(1024)(128)(4,1)} %bitcast.80), calls=%async_computation.2 | async-start | bytes 8388608
  790.9 30.8 %collective-permute-start.7 = (f32[5760]{0:T(1024)S(1)}, f32[5760]{0:T(1024)S(1)}, u32[]{:S(2)}, u32[]{:S(2)}) collective-permute-start(f32[5760]{0:T(1024)S(1)} %constant_dynamic-update-slice_fusion.5), channel_id=1, source_target_pairs={{0,1},{1,0},{2,3},{3,2},{4,5},{5,4},{6,7},{7,6}} | collective-permute-start | bytes 69128 | tf_op jit(solution)/shard_map/ppermute | solution.py:531
  799.3 24.1 %collective-permute-start.9 = (bf16[576,2048]{1,0:T(8,128)(2,1)S(1)}, bf16[576,2048]{1,0:T(8,128)(2,1)}, u32[]{:S(2)}, u32[]{:S(2)}) collective-permute-start(bf16[576,2048]{1,0:T(8,128)(2,1)S(1)} %add_convert_fusion.2), channel_id=1, source_target_pairs={{0,1},{1,0},{2,3},{3,2},{4,5},{5,4},{6,7},{7,6}} | collective-permute-start | bytes 7077896 | tf_op jit(solution)/shard_map/ppermute | solution.py:531

commit v2 on v1

v2 whole, which is shorter than its diff:
```python
import functools
import jax
import jax.numpy as jnp
from jax import lax
from jax.experimental import pallas as pl
from jax.experimental.pallas import tpu as pltpu
from jax.sharding import PartitionSpec as P

GRID = 64
POOL = 4
SIDE = GRID // POOL
BLOCK = SIDE * SIDE
EPS = 1e-6
ROPE_BASE = 1000000.0
ROPE_SCALE = 8.0
NEG_BIG = -1e30
HEAD = 256
HALF = HEAD // 2
BF = 256
RB = 256
VMEM_LIMIT = 60 * 1024 * 1024
F32 = jnp.float32
ZERO = 0
ALL = Ellipsis
BF16 = jnp.bfloat16


def params(sem):
    return pltpu.CompilerParams(dimension_semantics=sem, vmem_limit_bytes=VMEM_LIMIT)


def cost(flops, nbytes):
    return pl.CostEstimate(flops=int(flops), bytes_accessed=int(nbytes), transcendentals=0)


def dot(a, b):
    return jnp.dot(a, b, preferred_element_type=F32)


def dot_t(a, b):
    return lax.dot_general(a, b, (((1,), (1,)), ((), ())), preferred_element_type=F32)


def col_sum(v):
    return jnp.sum(v, axis=0, keepdims=True)


def row_mean(v):
    return jnp.mean(v, axis=-1, keepdims=True)


def iota(shape, axis):
    return lax.broadcasted_iota(jnp.int32, shape, axis)


def pool_kernel(vis_ref, out_ref):
    rows, cols = SIDE, POOL * GRID
    patch = iota((rows, cols), 1) % GRID
    sel = (patch // POOL == iota((rows, cols), 0)).astype(BF16)
    for i in range(vis_ref.shape[1] // cols):
        total = dot(sel, vis_ref[0, i * cols:(i + 1) * cols, :])
        out_ref[i * rows:(i + 1) * rows, :] = (total / (POOL * POOL)).astype(BF16)


def pool_patches(vis_loc):
    n_img, n_patch, dim = vis_loc.shape
    bands = 4
    steps = SIDE // bands
    return pl.pallas_call(
        pool_kernel,
        out_shape=jax.ShapeDtypeStruct((n_img * BLOCK, dim), BF16),
        grid=(n_img, steps),
        in_specs=[pl.BlockSpec((1, bands * POOL * GRID, dim), lambda n, i: (n, i, 0))],
        out_specs=pl.BlockSpec((bands * SIDE, dim), lambda n, i: (n * steps + i, 0)),
        compiler_params=params(("arbitrary", "arbitrary")),
        cost_estimate=cost(4e9, n_img * n_patch * dim * 2),
        name="pool",
    )(vis_loc)


def unpool_kernel(d_ref, out_ref):
    sel = (iota((GRID, SIDE), 0) // POOL == iota((GRID, SIDE), 1)).astype(BF16)
    for i in range(out_ref.shape[1] // (POOL * GRID)):
        band = (d_ref[i * SIDE:(i + 1) * SIDE, :].astype(F32) / (POOL * POOL)).astype(BF16)
        line = dot(sel, band).astype(BF16)
        for j in range(POOL):
            at = (i * POOL + j) * GRID
            out_ref[0, at:at + GRID, :] = line


def unpool_grad(d_pooled, n_img):
    dim = d_pooled.shape[1]
    bands = 4
    steps = SIDE // bands
    return pl.pallas_call(
        unpool_kernel,
        out_shape=jax.ShapeDtypeStruct((n_img, GRID * GRID, dim), BF16),
        grid=(n_img, steps),
        in_specs=[pl.BlockSpec((bands * SIDE, dim), lambda n, i: (n * steps + i, 0))],
        out_specs=pl.BlockSpec((1, bands * POOL * GRID, dim), lambda n, i: (n, i, 0)),
        compiler_params=params(("arbitrary", "arbitrary")),
        cost_estimate=cost(4e9, n_img * GRID * GRID * dim * 2),
        name="unpool",
    )(d_pooled)


def rms(x):
    return lax.rsqrt(row_mean(x * x) + EPS)


def norm_rope(raw, gain1, cos_t, sin_t):
    x = raw.astype(F32)
    x = x * rms(x) * gain1
    lo, hi = x[:, :HALF], x[:, HALF:]
    return (lo * cos_t - hi * sin_t).astype(BF16), (hi * cos_t + lo * sin_t).astype(BF16)


def norm_rope_grad(d_out, raw, gain1, cos_t, sin_t):
    d = d_out.astype(F32)
    lo, hi = d[:, :HALF], d[:, HALF:]
    d = jnp.concatenate([lo * cos_t + hi * sin_t, hi * cos_t - lo * sin_t], axis=1)
    x = raw.astype(F32)
    r = rms(x)
    xr = x * r
    dg = d * gain1
    d_raw = r * (dg - xr * row_mean(xr * dg))
    return d_raw.astype(BF16), col_sum(d * xr)


def qkv_kernel(n_text, meta, *refs):
    texts, refs = refs[:n_text], refs[n_text:]
    softs, refs = refs[:4], refs[4:]
    pre1, wq, wk, wv, qg1, kg1, cos_ref, sin_ref = refs[:8]
    x_out, hid_out, qraw_out, q_out, kraw_out, kv_out, x_scr = refs[-7:]
    i = pl.program_id(0)
    c = meta[0, 0] + i if n_text == 1 else meta[0, 1] + i
    if n_text == 1:
        x_scr[ALL] = texts[0][ALL]
    else:
        @pl.when(i == 0)
        def _():
            x_scr[ALL] = texts[0][ALL]

        @pl.when(i > 0)
        def _():
            x_scr[ALL] = texts[1][ALL]

    for slot in (0, 1):
        off = meta[2 + 3 * slot, c]
        for kind in (0, 1):
            soft = softs[2 * slot + kind]

            @pl.when((off < RB) & (meta[3 + 3 * slot, c] == kind))
            def _():
                src = iota((RB, BLOCK), 0) - off
                pick = (src == iota((RB, BLOCK), 1)).astype(BF16)
                row = iota((RB, 1), 0) - off
                inside = (row >= 0) & (row < BLOCK)
                x_scr[ALL] = jnp.where(inside, dot(pick, soft[ALL]).astype(BF16), x_scr[ALL])

    x_out[ALL] = x_scr[ALL]
    x = x_scr[ALL].astype(F32)
    hid_out[ALL] = (x * rms(x) * pre1[ALL]).astype(BF16)
    hid = hid_out[ALL]
    kraw_out[ALL] = dot(hid, wk[ALL]).astype(BF16)
    kv_out[:, HEAD:] = dot(hid, wv[ALL]).astype(BF16)
    cos_t, sin_t = cos_ref[ALL], sin_ref[ALL]
    lo, hi = norm_rope(kraw_out[ALL], kg1[ALL], cos_t, sin_t)
    kv_out[:, :HALF] = lo
    kv_out[:, HALF:HEAD] = hi
    for h in range(q_out.shape[1] // HEAD):
        raw = dot(hid, wq[:, h * HEAD:(h + 1) * HEAD]).astype(BF16)
        qraw_out[:, h * HEAD:(h + 1) * HEAD] = raw
        lo, hi = norm_rope(raw, qg1[ALL], cos_t, sin_t)
        q_out[:, h * HEAD:h * HEAD + HALF] = (lo * 0.0625).astype(BF16)
        q_out[:, h * HEAD + HALF:(h + 1) * HEAD] = (hi * 0.0625).astype(BF16)


def qkv_call(meta, texts, softs, pre1, wq, wk, wv, qg1, kg1, cos_t, sin_t, prev=()):
    rows = sum(t.shape[0] for t in texts)
    dim = texts[0].shape[1]
    steps = rows // RB
    width = wq.shape[1]
    side = 0 if len(texts) == 1 else 1

    def row(w):
        return pl.BlockSpec((RB, w), lambda i, meta: (meta[0, side] + i, 0))

    def whole(a):
        return pl.BlockSpec(a.shape, lambda i, meta: (0,) * a.ndim, pipeline_mode=pl.Buffered(1))

    def soft_spec(slot, kind):
        def index(i, meta):
            c = meta[0, side] + i
            return jnp.where(meta[3 + 3 * slot, c] == kind, meta[1 + 3 * slot, c], 0), 0

        return pl.BlockSpec((BLOCK, dim), index)

    def struct(w):
        return jax.ShapeDtypeStruct((2 * rows, w), BF16)

    if side == 0:
        text_specs = [pl.BlockSpec((RB, dim), lambda i, meta: (i, ZERO))]
    else:
        text_specs = [pl.BlockSpec((RB, dim), lambda i, meta: (ZERO, ZERO)),
                      pl.BlockSpec((RB, dim), lambda i, meta: (jnp.maximum(i - 1, 0), 0))]
    n_in = 1 + len(texts) + 4 + 8
    return pl.pallas_call(
        functools.partial(qkv_kernel, len(texts)),
        out_shape=[struct(dim), struct(dim), struct(width), struct(width), struct(HEAD), struct(2 * HEAD)],
        grid_spec=pltpu.PrefetchScalarGridSpec(
            num_scalar_prefetch=1, grid=(steps,),
            in_specs=text_specs + [soft_spec(ZERO, ZERO), soft_spec(0, 1), soft_spec(1, 0), soft_spec(1, 1)]
            + [whole(pre1), whole(wq), whole(wk), whole(wv), whole(qg1), whole(kg1), row(HALF), row(HALF)]
            + [pl.BlockSpec(memory_space=pl.ANY)] * len(prev),
            out_specs=[row(dim), row(dim), row(width), row(width), row(HEAD), row(2 * HEAD)],
            scratch_shapes=[pltpu.VMEM((RB, dim), BF16)]),
        input_output_aliases={n_in + k: k for k in range(len(prev))},
        compiler_params=params(("arbitrary",)),
        cost_estimate=cost(2 * rows * dim * (width + 2 * HEAD), 30e6),
        name="qkv",
    )(meta, *texts, softs[0], softs[1], softs[0], softs[1], pre1, wq, wk, wv, qg1, kg1, cos_t, sin_t, *prev)


def arrange_kernel(meta, mine, theirs, k_ref, v_ref, kt_ref, vt_ref):
    i = pl.program_id(0)

    def put(kv):
        k_ref[ALL] = kv[:, :HEAD]
        v_ref[ALL] = kv[:, HEAD:]
        kt_ref[ALL] = kv[:, :HEAD].astype(F32).T.astype(BF16)
        vt_ref[ALL] = kv[:, HEAD:].astype(F32).T.astype(BF16)

    @pl.when(meta[1, i] == 1)
    def _():
        put(mine[ALL])

    @pl.when(meta[1, i] == 0)
    def _():
        put(theirs[ALL])


def arrange_call(meta, mine, theirs):
    seq = 2 * mine.shape[0]
    blocks = meta.shape[1]
    rows = seq // blocks
    spec = lambda flag: pl.BlockSpec((rows, 2 * HEAD), lambda i, m: (jnp.where(m[1, i] == flag, m[0, i], 0), 0))
    tall = pl.BlockSpec((rows, HEAD), lambda i, m: (i, ZERO))
    flat = pl.BlockSpec((HEAD, rows), lambda i, m: (0, i))
    return pl.pallas_call(
        arrange_kernel,
        out_shape=[jax.ShapeDtypeStruct((seq, HEAD), BF16)] * 2 + [jax.ShapeDtypeStruct((HEAD, seq), BF16)] * 2,
        grid_spec=pltpu.PrefetchScalarGridSpec(
            num_scalar_prefetch=1, grid=(blocks,), in_specs=[spec(1), spec(0)], out_specs=[tall, tall, flat, flat]),
        compiler_params=params(("arbitrary",)),
        cost_estimate=cost(1e9, 12e6),
        name="arrange",
    )(meta, mine, theirs)


def fwd_kernel(span, q_ref, k_ref, vt_ref, lim_ref, o_ref, lse_ref, qt, acc, m_scr, l_scr):
    b = pl.program_id(0)
    heads = qt.shape[0]
    rows = q_ref.shape[0]
    for h in range(heads):
        qt[h] = q_ref[:, h * HEAD:(h + 1) * HEAD].astype(F32).T.astype(BF16)
    acc[ALL] = jnp.zeros_like(acc)
    m_scr[ALL] = jnp.full_like(m_scr, NEG_BIG)
    l_scr[ALL] = jnp.zeros_like(l_scr)

    def step(j, bk, masked):
        off = pl.multiple_of(j * bk, bk)
        keys = k_ref[pl.ds(off, bk), :]
        vals = vt_ref[:, pl.ds(off, bk)]
        if masked:
            seen = off + iota((bk, rows), 0) < lim_ref[ALL]
        for h in range(heads):
            s = dot(keys, qt[h])
            if masked:
                s = jnp.where(seen, s, NEG_BIG)
            m_old = m_scr[h]
            m_new = jnp.maximum(m_old, jnp.max(s, axis=0, keepdims=True))
            p = jnp.exp(s - m_new)
            alpha = jnp.exp(m_old - m_new)
            l_scr[h] = alpha * l_scr[h] + col_sum(p)
            m_scr[h] = m_new
            acc[h] = acc[h] * alpha + dot(vals, p.astype(BF16))

    @pl.loop(0, span[0, b])
    def _(j):
        step(j, 4 * BF, False)

    @pl.loop(span[1, b], span[2, b])
    def _(j):
        step(j, 2 * BF, False)

    @pl.loop(span[3, b], span[4, b])
    def _(j):
        step(j, BF, True)

    for h in range(heads):
        o_ref[:, h * HEAD:(h + 1) * HEAD] = (acc[h] / l_scr[h]).T.astype(BF16)
        lse_ref[h] = m_scr[h] + jnp.log(l_scr[h])


def fwd_call(span, q, k, vt, lim):
    rows, width = q.shape
    heads = width // HEAD
    seq = k.shape[0]
    wide = pl.BlockSpec((BF, width), lambda b, s: (b, 0))
    return pl.pallas_call(
        fwd_kernel,
        out_shape=[jax.ShapeDtypeStruct((rows, width), BF16), jax.ShapeDtypeStruct((heads, 1, rows), F32)],
        grid_spec=pltpu.PrefetchScalarGridSpec(
            num_scalar_prefetch=1, grid=(rows // BF,),
            in_specs=[wide, pl.BlockSpec((seq, HEAD), lambda b, s: (ZERO, ZERO)), pl.BlockSpec((HEAD, seq), lambda b, s: (ZERO, ZERO)),
                      pl.BlockSpec((1, BF), lambda b, s: (ZERO, b))],
            out_specs=[wide, pl.BlockSpec((heads, 1, BF), lambda b, s: (0, 0, b))],
            scratch_shapes=[pltpu.VMEM((heads, HEAD, BF), BF16), pltpu.VMEM((heads, HEAD, BF), F32),
                            pltpu.VMEM((heads, 1, BF), F32), pltpu.VMEM((heads, 1, BF), F32)]),
        compiler_params=params(("arbitrary",)),
        cost_estimate=cost(2 * rows * seq * width, 30e6),
        name="attn_fwd",
    )(span, q, k, vt, lim)


def bwd_kernel(span, q_ref, do_ref, k_ref, kt_ref, v_ref, lim_ref, lse_ref, delta_ref, qraw_ref, qg1, cos_ref, sin_ref,
               dq_mine, dq_theirs, gq_ref, dkv_mine, dkv_theirs, qt, dot_scr, dqt, dk_scr, dv_scr):
    b, h = pl.program_id(0), pl.program_id(1)
    heads = pl.num_programs(1)
    bq = q_ref.shape[0]
    mid = bq // 2

    @pl.when((b == 0) & (h == 0))
    def _():
        dk_scr[ALL] = jnp.zeros_like(dk_scr)
        dv_scr[ALL] = jnp.zeros_like(dv_scr)
        gq_ref[ALL] = jnp.zeros_like(gq_ref)

    qt[ALL] = q_ref[ALL].astype(F32).T.astype(BF16)
    dot_scr[ALL] = do_ref[ALL].astype(F32).T.astype(BF16)
    dqt[ALL] = jnp.zeros_like(dqt)

    def step(off, bk, masked, lo, hi):
        off = pl.multiple_of(off, bk)
        rows = pl.ds(off, bk)
        c = slice(lo, hi)
        p = jnp.exp(dot(k_ref[rows, :], qt[:, c]) - lse_ref[0][:, c])
        if masked:
            p = jnp.where(off + iota(p.shape, 0) < lim_ref[:, c], p, 0.0)
        ds = (p * (dot(v_ref[rows, :], dot_scr[:, c]) - delta_ref[0][:, c])).astype(BF16)
        dv_scr[rows, :] += dot(p.astype(BF16), do_ref[c, :])
        dk_scr[rows, :] += dot(ds, q_ref[c, :])
        dqt[:, c] += dot(kt_ref[:, rows], ds)

    base = span[0, b] * mid

    @pl.loop(0, span[0, b])
    def _(j):
        step(j * mid, mid, False, 0, bq)

    step(base, mid, True, 0, bq)
    step(base + mid, mid, True, mid, bq)

    @pl.when(span[1, b] == 1)
    def _():
        step(base + mid, BLOCK, True, mid - BLOCK, mid)

    @pl.when(span[2, b] == 1)
    def _():
        step(base + bq, BLOCK, True, bq - BLOCK, bq)

    d_q = (dqt[ALL].T * 0.0625).astype(BF16)
    d_raw, g_part = norm_rope_grad(d_q, qraw_ref[ALL], qg1[ALL], cos_ref[ALL], sin_ref[ALL])
    gq_ref[ALL] += g_part

    @pl.when(h < heads // 2)
    def _():
        dq_mine[ALL] = d_raw

    @pl.when(h >= heads // 2)
    def _():
        dq_theirs[ALL] = d_raw

    @pl.when((b == pl.num_programs(0) - 1) & (h == heads - 1))
    def _():
        for kind, out in ((0, dkv_mine), (1, dkv_theirs)):
            for part in (0, 1):
                src = pl.ds(pl.multiple_of(span[3 + kind, part] * bq, bq), bq)
                dst = slice(part * bq, (part + 1) * bq)
                out[dst, :HEAD] = dk_scr[src, :]
                out[dst, HEAD:] = dv_scr[src, :]


def bwd_call(span, q, d_o, k, kt, v, lim, lse, delta, q_raw, qg1, cos_t, sin_t):
    rows, width = q.shape
    heads = width // HEAD
    seq = v.shape[0]
    bq = rows // 2
    head = lambda h, s: (h + s[5, 0]) % heads
    tile = pl.BlockSpec((bq, HEAD), lambda b, h, s: (b, head(h, s)))
    fixed = lambda shape: pl.BlockSpec(shape, lambda b, h, s: (ZERO, ZERO))
    keys = pl.BlockSpec((seq, HEAD), lambda b, h, s: (ZERO, ZERO), pipeline_mode=pl.Buffered(1))
    stat = pl.BlockSpec((1, 1, bq), lambda b, h, s: (head(h, s), 0, b))
    rot = pl.BlockSpec((bq, HALF), lambda b, h, s: (b, 0))
    struct = jax.ShapeDtypeStruct
    return pl.pallas_call(
        bwd_kernel,
        out_shape=[struct((rows, width // 2), BF16), struct((rows, width // 2), BF16), struct((1, HEAD), F32),
                   struct((rows, 2 * HEAD), F32), struct((rows, 2 * HEAD), F32)],
        grid_spec=pltpu.PrefetchScalarGridSpec(
            num_scalar_prefetch=1, grid=(2, heads),
            in_specs=[tile, tile, keys, pl.BlockSpec((HEAD, seq), lambda b, h, s: (ZERO, ZERO), pipeline_mode=pl.Buffered(1)), keys,
                      pl.BlockSpec((1, bq), lambda b, h, s: (ZERO, b)), stat, stat, tile, fixed((1, HEAD)), rot, rot],
            out_specs=[pl.BlockSpec((bq, HEAD), lambda b, h, s: (b, jnp.minimum(h, heads // 2 - 1))),
                       pl.BlockSpec((bq, HEAD), lambda b, h, s: (b, jnp.maximum(h - heads // 2, 0))),
                       fixed((1, HEAD)), fixed((rows, 2 * HEAD)), fixed((rows, 2 * HEAD))],
            scratch_shapes=[pltpu.VMEM((HEAD, bq), BF16), pltpu.VMEM((HEAD, bq), BF16), pltpu.VMEM((HEAD, bq), F32),
                            pltpu.VMEM((seq, HEAD), F32), pltpu.VMEM((seq, HEAD), F32)]),
        compiler_params=params(("arbitrary", "arbitrary")),
        cost_estimate=cost(5 * rows * seq * width, 50e6),
        name="attn_bwd",
    )(span, q, d_o, k, kt, v, lim, lse, delta, q_raw, qg1, cos_t, sin_t)


def out_kernel(meta, o_ref, x_ref, dy_own, dy_mate, wo, post1,
               y_ref, da_ref, do_ref, delta_ref, gpost_ref, o_mine, o_theirs):
    i = pl.program_id(0)
    half = pl.num_programs(0) // 2
    own = (i < half) == (meta[0, 0] == 0)
    parts = [slice(k * RB, (k + 1) * RB) for k in range(o_ref.shape[0] // RB)]
    a_all = [dot(o_ref[c, :], wo[ALL]).astype(BF16) for c in parts]
    g_post = jnp.where(i == 0, jnp.zeros_like(gpost_ref[ALL]), gpost_ref[ALL])
    for c, a_lo in zip(parts, a_all):
        a = a_lo.astype(F32)
        ar = a * rms(a)
        y = x_ref[c, :].astype(F32) + ar * post1[ALL]

        @pl.when(own)
        def _():
            y_ref[c, :] = y.astype(BF16)

    for c, a_lo in zip(parts, a_all):
        a = a_lo.astype(F32)
        r = rms(a)
        ar = a * r
        dy = jnp.where(own, dy_own[c, :], dy_mate[c, :]).astype(F32)
        g_post = g_post + col_sum(dy * ar)
        dg = dy * post1[ALL]
        da_ref[c, :] = (r * (dg - ar * row_mean(ar * dg))).astype(BF16)
        do_ref[c, :] = dot_t(da_ref[c, :], wo[ALL]).astype(BF16)
        cols = []
        for h in range(o_ref.shape[1] // HEAD):
            d = slice(h * HEAD, (h + 1) * HEAD)
            cols.append(jnp.sum(do_ref[c, d].astype(F32) * o_ref[c, d].astype(F32), axis=-1, keepdims=True))
        delta_ref[c, :] = jnp.concatenate(cols, axis=1)
    gpost_ref[ALL] = g_post
    for kind, out in enumerate((o_mine, o_theirs)):
        width = out.shape[1]
        at = pl.multiple_of(((meta[0, 2] ^ kind) * 2 + meta[0, 3]) * width, width)
        out[ALL] = o_ref[:, pl.ds(at, width)]


def split_cols(first, src, mine, theirs):
    cut = src.shape[1] // 2

    @pl.when(first)
    def _():
        mine[ALL] = src[:, :cut]
        theirs[ALL] = src[:, cut:]

    @pl.when(jnp.logical_not(first))
    def _():
        mine[ALL] = src[:, cut:]
        theirs[ALL] = src[:, :cut]


def own_maps(half):
    def own_map(i, meta):
        is_lo = meta[0, 0] == 0
        return jnp.where(is_lo, jnp.minimum(i, half - 1), jnp.maximum(i - half, 0)), 0

    def mate_map(i, meta):
        is_lo = meta[0, 0] == 0
        return jnp.where(is_lo, jnp.maximum(i - half, 0), jnp.minimum(i, half - 1)), 0

    return own_map, mate_map


def out_call(meta, o, x, dy_own, dy_mate, wo, post1):
    rows, width = o.shape
    dim = wo.shape[1]
    step = 2 * RB
    steps = rows // step
    own_map, mate_map = own_maps(steps // 2)
    row = lambda w: pl.BlockSpec((step, w), lambda i, meta: (i, ZERO))
    gain = pl.BlockSpec((1, dim), lambda i, meta: (ZERO, ZERO))
    struct = lambda w: jax.ShapeDtypeStruct((rows, w), BF16)
    heads = width // HEAD
    return pl.pallas_call(
        out_kernel,
        out_shape=[jax.ShapeDtypeStruct(dy_own.shape, BF16), struct(dim), struct(width),
                   jax.ShapeDtypeStruct((rows, heads), F32), jax.ShapeDtypeStruct((1, dim), F32),
                   struct(width // 4), struct(width // 4)],
        grid_spec=pltpu.PrefetchScalarGridSpec(
            num_scalar_prefetch=1, grid=(steps,),
            in_specs=[row(width), row(dim), pl.BlockSpec((step, dim), own_map), pl.BlockSpec((step, dim), mate_map),
                      pl.BlockSpec(wo.shape, lambda i, meta: (ZERO, ZERO), pipeline_mode=pl.Buffered(1)), gain],
            out_specs=[pl.BlockSpec((step, dim), own_map), row(dim), row(width), row(heads), gain,
                       row(width // 4), row(width // 4)]),
        compiler_params=params(("arbitrary",)),
        cost_estimate=cost(4 * rows * dim * width, 60e6),
        name="out_proj",
    )(meta, o, x, dy_own, dy_mate, wo, post1)


def hid_kernel(meta, dq_mine, dq_theirs, dkv_mine, dkv_theirs, kraw_ref, cos_ref, sin_ref, kg1, wq_mine, wq_theirs, wk, wv, x_ref,
               pre1, dy_own, dy_mate, lim_ref, dtext_ref, dm_ref, dk_ref, dv_ref, gpre_ref, gk_ref):
    i = pl.program_id(0)
    half = pl.num_programs(0) // 2
    own = (i < half) == (meta[0, 0] == 0)
    g_pre = jnp.where(i == 0, jnp.zeros_like(gpre_ref[ALL]), gpre_ref[ALL])
    g_k = jnp.where(i == 0, jnp.zeros_like(gk_ref[ALL]), gk_ref[ALL])
    d_k = (dkv_mine[:, :HEAD] + dkv_theirs[:, :HEAD]).astype(BF16)
    dv_ref[ALL] = (dkv_mine[:, HEAD:] + dkv_theirs[:, HEAD:]).astype(BF16)
    dk_ref[ALL], g_part = norm_rope_grad(d_k, kraw_ref[ALL], kg1[ALL], cos_ref[ALL], sin_ref[ALL])
    gk_ref[ALL] = g_k + g_part
    parts = [slice(k * RB, (k + 1) * RB) for k in range(x_ref.shape[0] // RB)]
    dh_all = []
    for c in parts:
        dh = dot_t(dq_mine[c, :], wq_mine[ALL]) + dot_t(dq_theirs[c, :], wq_theirs[ALL])
        dh = dh + dot_t(dk_ref[c, :], wk[ALL]) + dot_t(dv_ref[c, :], wv[ALL])
        dh_all.append(dh.astype(BF16))
    for c, dh in zip(parts, dh_all):
        dh = dh.astype(F32)
        x = x_ref[c, :].astype(F32)
        r = rms(x)
        xr = x * r
        g_pre = g_pre + col_sum(dh * xr)
        dg = dh * pre1[ALL]
        dx = (r * (dg - xr * row_mean(xr * dg))).astype(BF16).astype(F32)
        dm_ref[c, :] = (jnp.where(own, dy_own[c, :], dy_mate[c, :]).astype(F32) + dx).astype(BF16)
    gpre_ref[ALL] = g_pre

    @pl.when(own)
    def _():
        dtext_ref[ALL] = jnp.where(lim_ref[:, :1] > 0, jnp.zeros_like(dm_ref[ALL]), dm_ref[ALL])


def hid_call(meta, dq_mine, dq_theirs, dkv_mine, dkv_theirs, k_raw, cos_t, sin_t, kg1, wq, wk, wv, x, pre1, dy_own, dy_mate, img_flag):
    rows = x.shape[0]
    dim, width = wq.shape
    cut = width // 2
    step = 2 * RB
    steps = rows // step
    own_map, mate_map = own_maps(steps // 2)
    row = lambda w: pl.BlockSpec((step, w), lambda i, meta: (i, ZERO))
    half_w = lambda flip: pl.BlockSpec((dim, cut), lambda i, meta: (0, meta[0, 2] ^ flip), pipeline_mode=pl.Buffered(1))
    whole = lambda a: pl.BlockSpec(a.shape, lambda i, meta: (ZERO, ZERO), pipeline_mode=pl.Buffered(1))
    return pl.pallas_call(
        hid_kernel,
        out_shape=[jax.ShapeDtypeStruct(dy_own.shape, BF16), jax.ShapeDtypeStruct((rows, dim), BF16),
                   jax.ShapeDtypeStruct((rows, HEAD), BF16), jax.ShapeDtypeStruct((rows, HEAD), BF16),
                   jax.ShapeDtypeStruct((1, dim), F32), jax.ShapeDtypeStruct((1, HEAD), F32)],
        grid_spec=pltpu.PrefetchScalarGridSpec(
            num_scalar_prefetch=1, grid=(steps,),
            in_specs=[row(cut), row(cut), row(2 * HEAD), row(2 * HEAD), row(HEAD), row(HALF), row(HALF), whole(kg1),
                      half_w(0), half_w(1), whole(wk), whole(wv), row(dim), whole(pre1),
                      pl.BlockSpec((step, dim), own_map), pl.BlockSpec((step, dim), mate_map), row(128)],
            out_specs=[pl.BlockSpec((step, dim), own_map), row(dim), row(HEAD), row(HEAD),
                       pl.BlockSpec((1, dim), lambda i, meta: (ZERO, ZERO)), pl.BlockSpec((1, HEAD), lambda i, meta: (ZERO, ZERO))]),
        compiler_params=params(("arbitrary",)),
        cost_estimate=cost(2 * rows * dim * (width + 2 * HEAD), 60e6),
        name="hid_bwd",
    )(meta, dq_mine, dq_theirs, dkv_mine, dkv_theirs, k_raw, cos_t, sin_t, kg1, wq, wq, wk, wv, x, pre1, dy_own, dy_mate, img_flag)


def pick_kernel(meta, mine0, theirs0, mine1, theirs1, out_ref, out_mine, out_theirs, blk):
    n = pl.program_id(0)
    off = meta[2, n]
    for slot, mine, theirs in ((0, mine0, theirs0), (1, mine1, theirs1)):
        is_mine = meta[3 + slot, n] == 1

        @pl.when(is_mine)
        def _():
            blk[ALL] = mine[ALL]

        @pl.when(jnp.logical_not(is_mine))
        def _():
            blk[ALL] = theirs[ALL]

        src = iota((BLOCK, RB), 0) + off - slot * RB
        pick = (src == iota((BLOCK, RB), 1)).astype(BF16)
        if slot == 0:
            out_ref[ALL] = dot(pick, blk[ALL]).astype(BF16)
        else:
            out_ref[ALL] = jnp.where(src[:, :1] >= 0, dot(pick, blk[ALL]).astype(BF16), out_ref[ALL])
    split_cols(meta[5, 0] == 0, out_ref, out_mine, out_theirs)


def pick_call(meta, mine, theirs):
    dim = mine.shape[1]
    n_img = meta.shape[1]
    at = lambda slot, kind: pl.BlockSpec((RB, dim), lambda n, meta: (jnp.where(meta[3 + slot, n] == kind, meta[slot, n], 0), 0))
    out = lambda w: pl.BlockSpec((BLOCK, w), lambda n, meta: (n, ZERO))
    struct = lambda w: jax.ShapeDtypeStruct((n_img * BLOCK, w), BF16)
    return pl.pallas_call(
        pick_kernel,
        out_shape=[struct(dim), struct(dim // 2), struct(dim // 2)],
        grid_spec=pltpu.PrefetchScalarGridSpec(
            num_scalar_prefetch=1, grid=(n_img,),
            in_specs=[at(0, 1), at(ZERO, ZERO), at(1, 1), at(1, 0)],
            out_specs=[out(dim), out(dim // 2), out(dim // 2)],
            scratch_shapes=[pltpu.VMEM((RB, dim), BF16)]),
        compiler_params=params(("arbitrary",)),
        cost_estimate=cost(4 * n_img * BLOCK * RB * dim, 20e6),
        name="pick_rows",
    )(meta, mine, theirs, mine, theirs)


def join_kernel(at_ref, *refs):
    pieces, out_ref = refs[:-1], refs[-1]
    for k, piece in enumerate(pieces):
        @pl.when(pl.program_id(0) == k)
        def _():
            out_ref[ALL] = piece[ALL]


def join_call(at, pieces, axis):
    rows, width = pieces[0].shape
    n = len(pieces)
    cuts = 2
    step = rows // cuts
    if axis == 0:
        shape = (n * rows, width)
        out = pl.BlockSpec((step, width), lambda h, i, at: (at[h] * cuts + i, 0))
    else:
        shape = (rows, n * width)
        out = pl.BlockSpec((step, width), lambda h, i, at: (i, at[h]))

    def spec(k):
        return pl.BlockSpec((step, width), lambda h, i, at: (jnp.where(h == k, i, jnp.where(h < k, 0, cuts - 1)), 0))

    return pl.pallas_call(
        join_kernel,
        out_shape=jax.ShapeDtypeStruct(shape, BF16),
        grid_spec=pltpu.PrefetchScalarGridSpec(
            num_scalar_prefetch=1, grid=(n, cuts), in_specs=[spec(k) for k in range(n)], out_specs=out),
        compiler_params=params(("arbitrary", "arbitrary")),
        cost_estimate=cost(1e9, 2 * n * rows * width * 2),
        name="join",
    )(at, *pieces)


def gain_norm(values, gain_vec):
    wide = values.astype(F32)
    return (wide * lax.rsqrt(row_mean(wide * wide) + EPS) * (1.0 + gain_vec)).astype(BF16)


def tdot(a, b):
    return lax.dot_general(a, b, (((0,), (0,)), ((), ())), preferred_element_type=F32)


def solution(mesh):
    n_dev = mesh.shape['cp']
    seq_spec = P(('dp', 'cp'))
    part_spec = P('dp')
    rep_spec = P()
    across = [(i, n_dev - 1 - i) for i in range(n_dev)]
    beside = [(i, i ^ 1) for i in range(n_dev)]

    def swap_x(v):
        return lax.ppermute(v, 'cp', across)

    def swap_c(v):
        return lax.ppermute(v, 'cp', beside)

    def device_body(vis_loc, text_loc, img_pos, grad_y, pn_gain, w_proj, pre_gain, w_query, w_key, w_value, q_gain, k_gain, w_out, post_gain):
        dev = lax.axis_index('cp')
        seq_loc, _ = text_loc.shape
        seq = seq_loc * n_dev
        mate = n_dev - 1 - dev
        lo_dev, hi_dev = jnp.minimum(dev, mate), jnp.maximum(dev, mate)
        is_lo = dev < mate
        chip = jnp.where(is_lo, 0, 1)
        my_set = lo_dev
        first = my_set == 0
        pre1 = (1.0 + pre_gain.astype(F32))[None]
        post1 = (1.0 + post_gain.astype(F32))[None]
        qg1 = (1.0 + q_gain.astype(F32))[None]
        kg1 = (1.0 + k_gain.astype(F32))[None]

        blocks = 2 * seq_loc // RB
        half = blocks // 2
        blk = jnp.arange(blocks)
        blk_base = jnp.where(blk < half, lo_dev * seq_loc + blk * RB, hi_dev * seq_loc + (blk - half) * RB)
        row = jnp.arange(2 * seq_loc)
        pos = jnp.where(row < seq_loc, lo_dev * seq_loc + row, (hi_dev - 1) * seq_loc + row)
        img = jnp.arange(img_pos.shape[0])
        img_dev = img // 2
        img_set = jnp.minimum(img_dev, n_dev - 1 - img_dev)
        img_slot = jnp.where(img_dev >= n_dev // 2, 2, 0) + img % 2
        img_kind = jnp.where(img_set == my_set, 0, 1)
        rel = img_pos[None, :] - blk_base[:, None]
        hit0 = (rel > -BLOCK) & (rel <= 0)
        hit1 = (rel > 0) & (rel < RB)
        of = lambda hit, v: jnp.sum(jnp.where(hit, v, 0), axis=1)
        off_of = lambda hit: jnp.where(jnp.any(hit, axis=1), of(hit, rel), seq)
        own_at = jnp.where(is_lo, 0, half)
        flags = jnp.where(blk == 0, own_at, jnp.where(blk == 1, half - own_at, jnp.where(blk == 2, my_set, chip)))
        meta = jnp.stack([flags, of(hit0, img_slot[None]), off_of(hit0), of(hit0, img_kind[None]),
                          of(hit1, img_slot[None]), off_of(hit1), of(hit1, img_kind[None])]).astype(jnp.int32)
        offset = pos[:, None] - img_pos[None, :]
        in_blk = (offset >= 0) & (offset < BLOCK)
        lim = jnp.maximum(pos + 1, jnp.max(jnp.where(in_blk, img_pos[None, :] + BLOCK, 0), axis=1)).astype(jnp.int32)
        is_img = jnp.any(in_blk, axis=1).astype(jnp.int32)
        f_end = jnp.max(lim.reshape(-1, BF), axis=1)
        f_base = blk_base if BF == RB else pos[::BF]
        f_span = jnp.stack([f_base // (4 * BF), f_base // (4 * BF) * 2, f_base // (2 * BF), f_base // (2 * BF) * 2,
                            (f_end + BF - 1) // BF]).astype(jnp.int32)
        half_end = jnp.max(lim.reshape(4, -1), axis=1)
        mid = seq_loc // 2
        mine_at = jnp.stack([lo_dev, hi_dev])
        their_at = jnp.stack([lo_dev ^ 1, hi_dev ^ 1])
        b_base = mine_at * seq_loc
        heads = w_query.shape[1] // HEAD
        b_span = jnp.stack([b_base // mid, half_end[0::2] > b_base + mid, half_end[1::2] > b_base + seq_loc, mine_at, their_at,
                            jnp.zeros_like(b_base) + my_set * (heads // 2)]).astype(jnp.int32)
        flag_w = jnp.broadcast_to(is_img[:, None], (2 * seq_loc, 128))
        dev_blk = jnp.arange(n_dev)
        kv_at = jnp.stack([jnp.where(dev_blk >= n_dev // 2, 1, 0),
                           jnp.minimum(dev_blk, n_dev - 1 - dev_blk) == my_set]).astype(jnp.int32)
        inv_freq = ROPE_BASE ** (-jnp.arange(0, HEAD, 2).astype(F32) / HEAD)
        angle = (pos.astype(F32) / ROPE_SCALE)[:, None] * inv_freq[None, :]
        cos_t, sin_t = jnp.cos(angle), jnp.sin(angle)
        halves_at = jnp.stack([my_set, 1 - my_set]).astype(jnp.int32)
        mine_q, their_q = 2 * my_set, 2 - 2 * my_set
        quarters_at = jnp.stack([mine_q + chip, mine_q + 1 - chip, their_q + chip, their_q + 1 - chip]).astype(jnp.int32)

        def quarters(piece, far, axis, after):
            far, _ = lax.optimization_barrier((far, after))
            return join_call(quarters_at, (piece, far, swap_c(piece), swap_c(far)), axis)

        def quarter_cols(v):
            return lax.dynamic_slice_in_dim(v, chip * (v.shape[1] // 2), v.shape[1] // 2, axis=1)


        text_mate0 = swap_x(text_loc[:RB])
        pooled_own = pool_patches(vis_loc)
        pooled_mate = swap_x(pooled_own)
        text_rest, _ = lax.optimization_barrier((text_loc[RB:], pooled_own))
        text_mate1 = swap_x(text_rest)
        dy_src, _ = lax.optimization_barrier((grad_y, text_mate1))
        dy_mate = swap_x(dy_src)

        n_own = pooled_own.shape[0]
        pooled = jnp.where(is_lo, jnp.concatenate([pooled_own, pooled_mate]), jnp.concatenate([pooled_mate, pooled_own]))
        normed, norm_pull = jax.vjp(gain_norm, pooled, pn_gain.astype(F32))
        soft = dot(normed, w_proj).astype(BF16)
        softs = (soft, swap_c(soft))
        normed_c = swap_c(normed)

        qkv_args = (pre1, w_query, w_key, w_value, qg1, kg1, cos_t, sin_t)
        first_rows = qkv_call(meta, (text_loc,), softs, *qkv_args)
        x, hidden, q_raw, q, k_raw, kv = qkv_call(meta, (text_mate0, text_mate1), softs, *qkv_args, prev=first_rows)
        k_all, v_all, kt_all, vt_all = arrange_call(kv_at, kv, swap_c(kv))
        hidden_c = swap_c(hidden)
        o, lse = fwd_call(f_span, q, k_all, vt_all, lim[None])
        y_loc, d_a, d_o, delta, g_post, o_mine, o_theirs = out_call(meta, o, x, grad_y, dy_mate, w_out, post1)
        o_c = swap_c(o_theirs)
        d_a_c = swap_c(d_a)
        delta_t = delta.T[:, None, :]
        dq_mine, dq_theirs, g_qg, dkv_mine, dkv_theirs = bwd_call(b_span, q, d_o, k_all, kt_all, v_all, lim[None], lse, delta_t, q_raw, qg1, cos_t, sin_t)
        dkv_c = swap_c(dkv_theirs)
        dq_c = swap_c(quarter_cols(dq_theirs))
        g_out_q = (tdot(o_mine, d_a) + tdot(o_c, d_a_c)).astype(BF16)
        g_query_q = (tdot(hidden, quarter_cols(dq_mine)) + tdot(hidden_c, dq_c)).astype(BF16)
        dkv_mine, g_out_q, g_query_q = lax.optimization_barrier((dkv_mine, g_out_q, g_query_q))
        g_out_far = swap_x(g_out_q)
        g_query_far = swap_x(g_query_q)
        grad_text, d_merged, dk_raw, d_v, g_pre, g_kg = hid_call(
            meta, dq_mine, dq_theirs, dkv_mine, dkv_c, k_raw, cos_t, sin_t, kg1, w_query, w_key, w_value, x, pre1, grad_y, dy_mate,
            flag_w)

        d_merged_c = swap_c(d_merged)
        kv_c = swap_c(jnp.where(first, d_v, dk_raw))
        g_kv = (tdot(hidden, jnp.where(first, dk_raw, d_v)) + tdot(hidden_c, kv_c)).astype(BF16)
        g_kv_c = swap_c(g_kv)
        g_key, g_value = jnp.where(first, g_kv, g_kv_c), jnp.where(first, g_kv_c, g_kv)

        my_img = jnp.concatenate([2 * lo_dev + jnp.arange(2), 2 * hi_dev + jnp.arange(2)])
        start = img_pos[my_img]
        blk0 = start // RB
        blk1 = jnp.minimum(blk0 + 1, seq // RB - 1)

        def locate(g):
            owner = g // half
            in_set = jnp.minimum(owner, n_dev - 1 - owner)
            return g % half + jnp.where(owner >= n_dev // 2, half, 0), in_set == my_set

        at0, mine0 = locate(blk0)
        at1, mine1 = locate(blk1)
        pick_meta = jnp.stack([at0, at1, start % RB, mine0, mine1, my_set + 0 * start]).astype(jnp.int32)
        d_soft, d_soft_mine, d_soft_theirs = pick_call(pick_meta, d_merged, d_merged_c)
        d_soft_c = swap_c(d_soft_theirs)
        d_normed = dot_t(d_soft, w_proj).astype(BF16)
        d_pooled, g_pn = norm_pull(d_normed)
        g_out = quarters(g_out_q, g_out_far, 0, d_soft)
        g_query = quarters(g_query_q, g_query_far, 1, d_pooled)
        d_own = jnp.where(is_lo, d_pooled[:n_own], d_pooled[n_own:])
        grad_vis = unpool_grad(d_own, vis_loc.shape[0])
        g_proj_half = (tdot(normed, d_soft_mine) + tdot(normed_c, d_soft_c)).astype(BF16)
        g_proj = join_call(halves_at, (g_proj_half, swap_c(g_proj_half)), 1)

        small = jnp.concatenate([g_pn, g_pre[0], g_qg[0], g_kg[0], g_post[0]])
        small = (small + swap_c(small)).astype(BF16)
        cuts = [g_pn.shape[0]]
        for g in (g_pre, g_qg, g_kg):
            cuts.append(cuts[-1] + g.shape[1])
        g_pn, g_pre, g_qg, g_kg, g_post = jnp.split(small, cuts)
        return (y_loc, grad_text, grad_vis, g_pn, g_proj, g_pre, g_query, g_key, g_value, g_qg, g_kg, g_out, g_post)

    in_specs = (seq_spec, seq_spec, part_spec, seq_spec) + (rep_spec,) * 10
    out_specs = (seq_spec, seq_spec, seq_spec) + (part_spec,) * 10

    return jax.shard_map(device_body, mesh=mesh, in_specs=in_specs, out_specs=out_specs, check_vma=False)
```

time: 839 us -> 725 us (0.86)
  other arithmetic: 84.5 us -> 25.9 us
  Pallas kernels: 487 us -> 444 us
  waiting for transfers between devices: 100 us -> 129 us
  local copies, waits for them, and re-layouts: 49.4 us -> 20.8 us
  matrix products: 95.4 us -> 69.8 us
  starting transfers between devices: 11.5 us -> 22.5 us
    pallas_call x1, Pallas kernels: 142 us -> 79.1 us  [fwd_call(): pl.pallas_call(fwd_kernel, out_shape=[jax.ShapeDtypeStruct((rows, width),...]
    select_n x12 -> x8, other arithmetic: 44.6 us -> 2.91 us  [the longest x1 1.45 us: device_body(): jnp.where(first, g_kv_c, g_kv)]
    pallas_call x3 -> x8, Pallas kernels: 226 us -> 245 us  [the longest x1 147 us: bwd_call(): pl.pallas_call(bwd_kernel, out_shape=[struct((rows, width // 2), BF16), s...]
    dot_general x5 -> x8, matrix products: 72.6 us -> 54.7 us  [tdot(): lax.dot_general(a, b, (((0,), (0,)), ((), ())), preferred_element_type=F32)]
    ppermute x3 -> x6, waiting for transfers between devices: 100 us -> 118 us  [swap_x(): return lax.ppermute(v, 'cp', across)]
    concatenate x3 -> x0, other arithmetic: 17.5 us -> none  [the longest x1 8.53 us: device_body(): soft_all = jnp.concatenate([soft, swap_c(soft)])]
    unnamed x67 -> x88, local copies, waits for them, and re-layouts: 22.9 us -> 7.26 us
    ppermute x14 -> x18, waiting for transfers between devices: 0.04 us -> 11.3 us  [swap_c(): return lax.ppermute(v, 'cp', beside)]
  transfers between devices with their start and end apart: 17 -> 24, of which waited for: 2 -> 6; matrix products, arithmetic and copies ran while one was open for 25% -> 13% of each run, Pallas kernels for 52% -> 50%
where the time goes in v2:
time: 725 us; the launch traced here: 714 us
  Pallas kernels  444 us (61%)
  waiting for transfers between devices  129 us (18%)
  matrix products  69.8 us (10%)
  other arithmetic  25.9 us (4%)
  starting transfers between devices  22.5 us (3%)
  local copies, waits for them, and re-layouts  20.8 us (3%)
    pallas_call x1, Pallas kernels, bwd_call(): pl.pallas_call(bwd_kernel, out_shape=[struct((rows, width // 2), BF16), s...  147 us
    ppermute x6, waiting for transfers between devices, swap_x(): return lax.ppermute(v, 'cp', across)  118 us
    pallas_call x1, Pallas kernels, fwd_call(): pl.pallas_call(fwd_kernel, out_shape=[jax.ShapeDtypeStruct((rows, width),...  79.1 us
    pallas_call x1, Pallas kernels, out_call(): pl.pallas_call(out_kernel, out_shape=[jax.ShapeDtypeStruct(dy_own.shape,...  56 us
    dot_general x8, matrix products, tdot(): lax.dot_general(a, b, (((0,), (0,)), ((), ())), preferred_element_type=F32)  54.7 us
    pallas_call x2, Pallas kernels, qkv_call(): pl.pallas_call(functools.partial(qkv_kernel, len(texts)), out_shape=[stru...  51.2 us
    pallas_call x1, Pallas kernels, hid_call(): pl.pallas_call(hid_kernel, out_shape=[jax.ShapeDtypeStruct(dy_own.shape,...  44.3 us
    pallas_call x3, Pallas kernels, join_call(): pl.pallas_call(join_kernel, out_shape=jax.ShapeDtypeStruct(shape, BF16),...  27.7 us
  transfers between devices with their start and end apart: 24, of which 6 were waited for; matrix products, arithmetic and copies ran while one was open for 13% of the time, Pallas kernels for 50%

profile of v2, /device:TPU:0, one launch (start us, length us, event | category | flops | bytes accessed | tf_op | source)
XLA Modules:
  0.0 714.2 jit_solution(1288741659620673356)
XLA Ops:
  0.7 10.4 %pool.1 = bf16[512,1152]{1,0:T(8,128)(2,1)} custom-call(bf16[2,4096,1152]{2,1,0:T(8,128)(2,1)} %vis_ref.1), custom_call_target="tpu_custom_call" | custom-call | flops 4000000000 | bytes 18874368 | tf_op jit(solution)/shard_map/pool/pallas_call | solution.py:69
  11.1 2.7 collective-permute-start.2
  13.8 26.6 %collective-permute-done.2 = bf16[512,1152]{1,0:T(8,128)(2,1)S(1)} collective-permute-done((bf16[512,1152]{1,0:T(8,128)(2,1)}, bf16[512,1152]{1,0:T(8,128)(2,1)S(1)}, u32[]{:S(2)}, u32[]{:S(2)}) %collective-permute-start.2) | collective-permute-done | bytes 1179680 | tf_op jit(solution)/shard_map/ppermute | solution.py:673
  40.5 2.9 fusion.5
  44.0 2.6 fusion.2
  46.6 7.1 convolution_convert_fusion.1.refs_1_.refs_3_.refs_2_.refs_4_
  53.9 2.1 slice.19
  56.0 2.4 collective-permute-start.1
  58.4 1.1 slice.18
  61.8 5.5 multiply_sine_fusion
  67.3 0.6 stack.115.meta
  67.9 24.2 %qkv.2 = (bf16[2048,2048]{1,0:T(8,128)(2,1)}, bf16[2048,2048]{1,0:T(8,128)(2,1)}, bf16[2048,2048]{1,0:T(8,128)(2,1)}, bf16[2048,2048]{1,0:T(8,128)(2,1)}, bf16[2...) custom-call(s32[7,8]{1,0:T(8,128)} %stack.115.meta, bf16[1024,2048]{1,0:T(8,128)(2,1)} %refs_0_.1, ...), custom_call_target="tpu_custom_call" | custom-call | flops 10737418240 | bytes 30000000 | tf_op jit(solution)/shard_map/qkv/pallas_call | solution.py:208
  92.1 57.4 %collective-permute-done.refs_0_ = bf16[256,2048]{1,0:T(8,128)(2,1)} collective-permute-done((bf16[256,2048]{1,0:T(8,128)(2,1)}, bf16[256,2048]{1,0:T(8,128)(2,1)}, u32[]{:S(2)}, u32[]{:S(2)}) %collective-permute-start) | collective-permute-done | bytes 1048608 | tf_op jit(solution)/shard_map/ppermute | solution.py:673
  149.5 1.7 copy-done.6
  151.2 27.0 %qkv.3 = (bf16[2048,2048]{1,0:T(8,128)(2,1)}, bf16[2048,2048]{1,0:T(8,128)(2,1)}, bf16[2048,2048]{1,0:T(8,128)(2,1)}, bf16[2048,2048]{1,0:T(8,128)(2,1)}, bf16[2...) custom-call(s32[7,8]{1,0:T(8,128)} %stack.115.meta, ...), custom_call_target="tpu_custom_call", output_to_operand_aliasing={{0}: (15, {}), {1}: (16, {}), {2}: (17, {}), {3}: (18, {}),... | custom-call | flops 10737418240 | bytes 30000000 | tf_op jit(solution)/shard_map/qkv/pallas_call | solution.py:208
  178.8 0.6 stack.116.span
  179.7 0.6 stack.134.span
  180.3 2.0 collective-permute-start.5
  182.9 0.6 convert_add_fusion
  183.5 0.6 fusion.14.lim_ref
  184.1 1.3 copy-done.10
  185.4 7.8 %arrange.1 = (bf16[4096,256]{1,0:T(8,128)(2,1)}, bf16[4096,256]{1,0:T(8,128)(2,1)}, bf16[256,4096]{1,0:T(8,128)(2,1)}, bf16[256,4096]{1,0:T(8,128)(2,1)}) custom-call(s32[2,4]{1,0:T(2,128)} %pad_add_fusion.meta, bf16[2048,512]{1,0:T(8,128)(2,1)} %get-tuple-element.67.mine, bf16[2048,512]{1,0:T(8,128)(2,1)} %copy-done.10), custom_call_target="tpu_custom_call" | custom-call | flops 1000000000 | bytes 12000000 | tf_op jit(solution)/shard_map/arrange/pallas_call | solution.py:250
  193.2 79.1 %attn_fwd.1 = (bf16[2048,2048]{1,0:T(8,128)(2,1)}, f32[8,1,2048]{2,1,0:T(1,128)}) custom-call(s32[5,8]{1,0:T(8,128)} %stack.116.span, bf16[2048,2048]{1,0:T(8,128)(2,1)} %get-tuple-element.66.q_ref, bf16[4096,256]{1,0:T(8,128)(2,1)} %get-tuple-element.68.k_ref, bf16[256,4096]{1,0:T(8,128)(2,1)} %get-tuple-element.69.vt_ref, s32[1,2048]{1,0:T(1,128)} %fusion.14.lim_ref), custom_call_target="tpu_custom_call" | custom-call | flops 34359738368 | bytes 30000000 | tf_op jit(solution)/shard_map/attn_fwd/pallas_call | solution.py:311
  272.3 1.0 collective-permute-done.5.dy_mate
  273.3 56.0 %out_proj.1 = (bf16[1024,2048]{1,0:T(8,128)(2,1)}, bf16[2048,2048]{1,0:T(8,128)(2,1)}, bf16[2048,2048]{1,0:T(8,128)(2,1)}, f32[2048,8]{1,0:T(8,128)}, f32[1,2048...) custom-call(s32[7,8]{1,0:T(8,128)} %stack.115.meta, bf16[2048,2048]{1,0:T(8,128)(2,1)} %get-tuple-element.70.o_ref, ...), custom_call_target="tpu_custom_call" | custom-call | flops 34359738368 | bytes 60000000 | tf_op jit(solution)/shard_map/out_proj/pallas_call | solution.py:500
  329.4 1.5 copy.41
  330.9 0.7 broadcast_in_dim.140.delta_ref
  331.6 1.9 collective-permute-start.7
  333.5 147.2 %attn_bwd.1 = (bf16[2048,1024]{1,0:T(8,128)(2,1)}, bf16[2048,1024]{1,0:T(8,128)(2,1)}, f32[1,256]{1,0:T(1,128)}, f32[2048,512]{1,0:T(8,128)}, f32[2048,512]{1,0:T(8,128)}) custom-call(s32[6,2]{1,0:T(8,128)} %stack.134.span, bf16[2048,2048]{1,0:T(8,128)(2,1)} %get-tuple-element.66.q_ref, bf16[2048,2048]{1,0:T(8,128)(2,1)} %get-tuple-element.74.do_ref, ...), custom_call_target="tpu_custom_call" | custom-call | flops 85899345920 | bytes 50000000 | tf_op jit(solution)/shard_map/attn_bwd/pallas_call | solution.py:407
  480.8 1.9 constant_dynamic-slice_fusion
  482.7 7.5 %collective-permute-start.9 = (bf16[2048,512]{1,0:T(8,128)(2,1)S(1)}, bf16[2048,512]{1,0:T(8,128)(2,1)S(1)}, u32[]{:S(2)}, u32[]{:S(2)}) collective-permute-start(bf16[2048,512]{1,0:T(8,128)(2,1)S(1)} %constant_dynamic-slice_fusion), channel_id=1, source_target_pairs={{0,1},{1,0},{2,3},{3,2},{4,5},{5,4},{6,7},{7,6}} | collective-permute-start | bytes 6291464 | tf_op jit(solution)/shard_map/ppermute | solution.py:676
  490.4 0.7 collective-permute-start.10
  491.1 2.9 collective-permute-done.9
  494.0 9.7 %fusion.35 = f32[2048,512]{1,0:T(8,128)} fusion(bf16[2048,2048]{1,0:T(8,128)(2,1)} %collective-permute-done.8, bf16[2048,512]{1,0:T(8,128)(2,1)S(1)} %collective-permute-done.9), kind=kOutput, calls=%fused_computation.164 | convolution fusion | flops 4294967296 | bytes 14680064 | tf_op jit(solution)/shard_map/dot_general | solution.py:661
  503.7 8.1 %add_convert_fusion.1.refs_0_ = bf16[2048,512]{1,0:T(8,128)(2,1)} fusion(f32[2048,512]{1,0:T(8,128)} %fusion.35, bf16[2048,2048]{1,0:T(8,128)(2,1)S(1)} %bitcast.105, bf16[2048,1024]{1,0:T(8,128)(2,1)} %get-tuple-element.80.dq_mine, s32[]{:T(128)S(6)} %select_n.444), kind=kOutput, calls=%fused_computation.16 | convolution fusion | flops 4297064448 | bytes 16777220 | tf_op jit(solution)/shard_map/dot_general | solution.py:661
  511.8 7.5 %fusion.34 = f32[512,2048]{1,0:T(8,128)S(1)} fusion(bf16[2048,512]{1,0:T(8,128)(2,1)S(1)} %collective-permute-done.6, bf16[2048,2048]{1,0:T(8,128)(2,1)} %collective-permute-done.7), kind=kOutput, calls=%fused_computation.163 | convolution fusion | flops 4294967296 | bytes 14680064 | tf_op jit(solution)/shard_map/dot_general | solution.py:661
  519.4 5.8 add_convert_fusion.2.refs_0_
  525.2 2.1 copy-done.29
  527.2 1.3 broadcast_in_dim.141.lim_ref
  528.5 44.3 %hid_bwd.1 = (bf16[1024,2048]{1,0:T(8,128)(2,1)}, bf16[2048,2048]{1,0:T(8,128)(2,1)}, bf16[2048,256]{1,0:T(8,128)(2,1)}, bf16[2048,256]{1,0:T(8,128)(2,1)}, f32[1,2048]{1,0:T(1,128)}, /*index=5*/f32[1,256]{1,0:T(1,128)}) custom-call(s32[7,8]{1,0:T(8,128)} %stack.115.meta, bf16[2048,1024]{1,0:T(8,128)(2,1)} %get-tuple-element.80.dq_mine, ...), custom_call_target="tpu_custom_call" | custom-call | flops 21474836480 | bytes 60000000 | tf_op jit(solution)/shard_map/hid_bwd/pallas_call | solution.py:560
  573.2 1.3 broadcast_select_fusion.2
  574.8 0.6 gather_fusion
  575.5 0.6 stack.135.meta
  576.1 0.6 pad_add_fusion.2.at_ref
  577.8 0.7 collective-permute-start.21
  578.4 1.1 collective-permute-start.16
  579.5 8.4 %collective-permute-done.19 = bf16[2048,256]{1,0:T(8,128)(2,1)} collective-permute-done((bf16[2048,256]{1,0:T(8,128)(2,1)S(1)}, bf16[2048,256]{1,0:T(8,128)(2,1)}, u32[]{:S(2)}, u32[]{:S(2)}) %collective-permute-start.19) | collective-permute-done | bytes 1048608 | tf_op jit(solution)/shard_map/ppermute | solution.py:676
  587.9 7.5 %fusion.37 = f32[2048,256]{1,0:T(8,128)} fusion(bf16[2048,2048]{1,0:T(8,128)(2,1)} %collective-permute-done.8, bf16[2048,256]{1,0:T(8,128)(2,1)} %collective-permute-done.19), kind=kOutput, calls=%fused_computation.166 | convolution fusion | flops 2147483648 | bytes 11534336 | tf_op jit(solution)/shard_map/dot_general | solution.py:661
  595.4 11.3 %pick_rows.1 = (bf16[1024,2048]{1,0:T(8,128)(2,1)}, bf16[1024,1024]{1,0:T(8,128)(2,1)}, bf16[1024,1024]{1,0:T(8,128)(2,1)}) custom-call(s32[6,4]{1,0:T(8,128)} %stack.135.meta, bf16[2048,2048]{1,0:T(8,128)(2,1)} %get-tuple-element.91.mine0.mine1, bf16[2048,2048]{1,0:T(8,128)(2,1)} %collective-permute-done.11.theirs0.theirs1, ...), custom_call_target="tpu_custom_call" | custom-call | flops 2147483648 | bytes 20000000 | tf_op jit(solution)/shard_map/pick_rows/pallas_call | solution.py:607
  606.7 0.6 collective-permute-start.14
  607.3 6.9 fusion.7
  614.5 7.9 %fusion.3 = (f32[1152]{0:T(1024)S(1)}, f32[1024]{0:T(1024)S(1)}, bf16[1024,1152]{1,0:T(8,128)(2,1)S(1)}) fusion(f32[1024]{0:T(1024)S(1)} %copy-done.17, bf16[512,1152]{1,0:T(8,128)(2,1)S(1)} %copy-done.2, bf16[512,1152]{1,0:T(8,128)(2,1)S(1)} %copy-done.4, pred[]{:T(512)S(6)} %lt.113, f32[1152]{0:T(1024)S(1)} %copy-done.13, ...), kind=kOutput, calls=%fused_computation.11 | convolution fusion | flops 4853069824 | bytes 13648897 | tf_op jit(solution)/shard_map/dot_general | solution.py:41
  623.0 5.2 fusion.36
  628.2 4.1 add_convert_fusion.refs_0_
  632.3 4.9 fusion.4
  637.7 33.0 %collective-permute-done.16.refs_1_ = bf16[2048,512]{1,0:T(8,128)(2,1)} collective-permute-done((bf16[2048,512]{1,0:T(8,128)(2,1)}, bf16[2048,512]{1,0:T(8,128)(2,1)}, u32[]{:S(2)}, u32[]{:S(2)}) %collective-permute-start.16) | collective-permute-done | bytes 2097184 | tf_op jit(solution)/shard_map/ppermute | solution.py:673
  671.3 1.5 broadcast_select_fusion
  672.7 1.1 slice_select_fusion.d_ref
  673.9 9.2 %unpool.1 = bf16[2,4096,1152]{2,1,0:T(8,128)(2,1)} custom-call(bf16[512,1152]{1,0:T(8,128)(2,1)} %slice_select_fusion.d_ref), custom_call_target="tpu_custom_call" | custom-call | flops 4000000000 | bytes 18874368 | tf_op jit(solution)/shard_map/unpool/pallas_call | solution.py:95
  684.2 0.6 fusion.32
  684.8 10.8 %join.5 = bf16[2048,2048]{1,0:T(8,128)(2,1)} custom-call(s32[4]{0:T(128)} %pad_add_fusion.3.at_ref, bf16[512,2048]{1,0:T(8,128)(2,1)} %add_convert_fusion.2.refs_0_, bf16[512,2048]{1,0:T(8,128)(2,1)} %collective-permute-done.21.refs_1_, bf16[512,2048]{1,0:T(8,128)(2,1)} %collective-permute-done.22.refs_2_, bf16[512,2048]{1,0:T(8,128)(2,1)} %collective-permute-done.23.refs_3_), custom_call_target="tpu_custom_call" | custom-call | flops 1000000000 | bytes 16777216 | tf_op jit(solution)/shard_map/join/pallas_call | solution.py:644
  695.6 10.8 %join.4 = bf16[2048,2048]{1,0:T(8,128)(2,1)} custom-call(s32[4]{0:T(128)} %pad_add_fusion.3.at_ref, bf16[2048,512]{1,0:T(8,128)(2,1)} %add_convert_fusion.1.refs_0_, bf16[2048,512]{1,0:T(8,128)(2,1)} %collective-permute-done.16.refs_1_, bf16[2048,512]{1,0:T(8,128)(2,1)} %collective-permute-done.17.refs_2_, bf16[2048,512]{1,0:T(8,128)(2,1)} %collective-permute-done.18.refs_3_), custom_call_target="tpu_custom_call" | custom-call | flops 1000000000 | bytes 16777216 | tf_op jit(solution)/shard_map/join/pallas_call | solution.py:644
  706.3 1.4 copy-done.9
  707.8 6.2 join.3
  (168 shorter events, 9.4 us)
Async XLA Ops:
  0.6 13.2 %copy-start.22 = (bf16[1152]{0:T(1024)(128)(2,1)S(1)}, bf16[1152]{0:T(1024)(128)(2,1)}, u32[]{:S(2)}) copy-start(bf16[1152]{0:T(1024)(128)(2,1)} %param.18) | copy-start | bytes 6916
  11.1 29.4 %collective-permute-start.2 = (bf16[512,1152]{1,0:T(8,128)(2,1)}, bf16[512,1152]{1,0:T(8,128)(2,1)S(1)}, u32[]{:S(2)}, u32[]{:S(2)}) collective-permute-start(bf16[512,1152]{1,0:T(8,128)(2,1)} %pool.1), channel_id=1, source_target_pairs={{0,3},{1,2},{2,1},{3,0},{4,7},{5,6},{6,5},{7,4}} | collective-permute-start | bytes 3538952 | tf_op jit(solution)/shard_map/ppermute | solution.py:673
  13.8 32.7 %copy-start.27 = (bf16[1152,2048]{1,0:T(8,128)(2,1)S(1)}, bf16[1152,2048]{1,0:T(8,128)(2,1)}, u32[]{:S(2)}) copy-start(bf16[1152,2048]{1,0:T(8,128)(2,1)} %param.19) | copy-start | bytes 14155780
  13.8 39.9 %copy-start.12 = (f32[1152]{0:T(1024)}, f32[1152]{0:T(1024)S(1)}, u32[]{:S(2)}) copy-start(f32[1152]{0:T(1024)S(1)} %convert_add_fusion.2) | copy-start | bytes 13828
  40.5 6.0 copy-start.3
  44.0 9.7 %copy-start.16 = (f32[1024]{0:T(1024)}, f32[1024]{0:T(1024)S(1)}, u32[]{:S(2)}) copy-start(f32[1024]{0:T(1024)S(1)} %fusion.21) | copy-start | bytes 12292
  46.6 7.2 %copy-start.7 = (bf16[1024,1152]{1,0:T(8,128)(2,1)}, bf16[1024,1152]{1,0:T(8,128)(2,1)S(1)}, u32[]{:S(2)}) copy-start(bf16[1024,1152]{1,0:T(8,128)(2,1)S(1)} %fusion.2) | copy-start | bytes 7077892
  46.6 7.3 %copy-start.5 = (bf16[1024,2048]{1,0:T(8,128)(2,1)S(1)}, bf16[1024,2048]{1,0:T(8,128)(2,1)}, u32[]{:S(2)}) copy-start(bf16[1024,2048]{1,0:T(8,128)(2,1)} %refs_0_.1) | copy-start | bytes 12582916
  53.7 5.8 copy-start
  53.7 6.3 copy-start.33
  53.8 6.8 copy-start.34
  53.8 7.4 %copy-start.23 = (bf16[2048]{0:T(1024)(128)(2,1)S(1)}, bf16[2048]{0:T(1024)(128)(2,1)}, u32[]{:S(2)}) copy-start(bf16[2048]{0:T(1024)(128)(2,1)} %param.20) | copy-start | bytes 12292
  53.8 14.1 %collective-permute-start.3 = (bf16[1024,2048]{1,0:T(8,128)(2,1)}, bf16[1024,2048]{1,0:T(8,128)(2,1)}, u32[]{:S(2)}, u32[]{:S(2)}) collective-permute-start(bf16[1024,2048]{1,0:T(8,128)(2,1)} %convolution_convert_fusion.1.refs_1_.refs_3_.refs_2_.refs_4_), channel_id=1, source_target_pairs={{0,1},{1,0},{2,3},{3,2},{4,5},{5,4},{6,7},{7,6}} | collective-permute-start | bytes 12582920 | tf_op jit(solution)/shard_map/ppermute | solution.py:676
  56.0 93.5 %collective-permute-start.1 = (bf16[768,2048]{1,0:T(8,128)(2,1)}, bf16[768,2048]{1,0:T(8,128)(2,1)S(1)}, u32[]{:S(2)}, u32[]{:S(2)}) collective-permute-start(bf16[768,2048]{1,0:T(8,128)(2,1)} %slice.19), channel_id=1, source_target_pairs={{0,3},{1,2},{2,1},{3,0},{4,7},{5,6},{6,5},{7,4}} | collective-permute-start | bytes 9437192 | tf_op jit(solution)/shard_map/ppermute | solution.py:673
  59.4 90.1 %collective-permute-start = (bf16[256,2048]{1,0:T(8,128)(2,1)}, bf16[256,2048]{1,0:T(8,128)(2,1)}, u32[]{:S(2)}, u32[]{:S(2)}) collective-permute-start(bf16[256,2048]{1,0:T(8,128)(2,1)} %slice.18), channel_id=1, source_target_pairs={{0,3},{1,2},{2,1},{3,0},{4,7},{5,6},{6,5},{7,4}} | collective-permute-start | bytes 3145736 | tf_op jit(solution)/shard_map/ppermute | solution.py:673
  59.5 118.7 %copy-start.14 = (s32[2048]{0:T(1024)}, s32[2048]{0:T(1024)S(1)}, u32[]{:S(2)}) copy-start(s32[2048]{0:T(1024)S(1)} %add_select_fusion) | copy-start | bytes 24580
  149.5 1.7 copy-start.6
  151.2 31.7 %copy-start.24 = (bf16[2048]{0:T(1024)(128)(2,1)S(1)}, bf16[2048]{0:T(1024)(128)(2,1)}, u32[]{:S(2)}) copy-start(bf16[2048]{0:T(1024)(128)(2,1)} %param.27) | copy-start | bytes 12292
  178.2 5.9 collective-permute-start.4
  180.3 93.0 %collective-permute-start.5 = (bf16[1024,2048]{1,0:T(8,128)(2,1)}, bf16[1024,2048]{1,0:T(8,128)(2,1)}, u32[]{:S(2)}, u32[]{:S(2)}) collective-permute-start(bf16[1024,2048]{1,0:T(8,128)(2,1)} %dy_own.3), channel_id=1, source_target_pairs={{0,3},{1,2},{2,1},{3,0},{4,7},{5,6},{6,5},{7,4}} | collective-permute-start | bytes 12582920 | tf_op jit(solution)/shard_map/ppermute | solution.py:673
  184.1 309.9 %collective-permute-start.8 = (bf16[2048,2048]{1,0:T(8,128)(2,1)}, bf16[2048,2048]{1,0:T(8,128)(2,1)}, u32[]{:S(2)}, u32[]{:S(2)}) collective-permute-start(bf16[2048,2048]{1,0:T(8,128)(2,1)} %get-tuple-element.86), channel_id=1, source_target_pairs={{0,1},{1,0},{2,3},{3,2},{4,5},{5,4},{6,7},{7,6}} | collective-permute-start | bytes 25165832 | tf_op jit(solution)/shard_map/ppermute | solution.py:676
  331.6 180.2 %collective-permute-start.7 = (bf16[2048,2048]{1,0:T(8,128)(2,1)}, bf16[2048,2048]{1,0:T(8,128)(2,1)}, u32[]{:S(2)}, u32[]{:S(2)}) collective-permute-start(bf16[2048,2048]{1,0:T(8,128)(2,1)} %get-tuple-element.84), channel_id=1, source_target_pairs={{0,1},{1,0},{2,3},{3,2},{4,5},{5,4},{6,7},{7,6}} | collective-permute-start | bytes 25165832 | tf_op jit(solution)/shard_map/ppermute | solution.py:676
  333.5 156.7 %copy-start.31 = (bf16[2048,512]{1,0:T(8,128)(2,1)S(1)}, bf16[2048,512]{1,0:T(8,128)(2,1)}, u32[]{:S(2)}) copy-start(bf16[2048,512]{1,0:T(8,128)(2,1)} %get-tuple-element.85) | copy-start | bytes 6291460
  480.8 9.4 %copy-start.1 = (s32[8]{0:T(128)S(1)}, s32[8]{0:T(128)}, u32[]{:S(2)}) copy-start(s32[8]{0:T(128)} %param.16) | copy-start | bytes 100
  480.8 9.4 %copy-start.15 = (s32[2048]{0:T(1024)S(1)}, s32[2048]{0:T(1024)}, u32[]{:S(2)}) copy-start(s32[2048]{0:T(1024)} %copy-done.14) | copy-start | bytes 24580
  480.8 9.6 %copy-start.28 = (f32[2048,512]{1,0:T(8,128)S(1)}, f32[2048,512]{1,0:T(8,128)}, u32[]{:S(2)}) copy-start(f32[2048,512]{1,0:T(8,128)} %get-tuple-element.88) | copy-start | bytes 12582916
  482.7 11.3 %collective-permute-start.9 = (bf16[2048,512]{1,0:T(8,128)(2,1)S(1)}, bf16[2048,512]{1,0:T(8,128)(2,1)S(1)}, u32[]{:S(2)}, u32[]{:S(2)}) collective-permute-start(bf16[2048,512]{1,0:T(8,128)(2,1)S(1)} %constant_dynamic-slice_fusion), channel_id=1, source_target_pairs={{0,1},{1,0},{2,3},{3,2},{4,5},{5,4},{6,7},{7,6}} | collective-permute-start | bytes 6291464 | tf_op jit(solution)/shard_map/ppermute | solution.py:676
  490.3 21.5 %collective-permute-start.6 = (bf16[2048,512]{1,0:T(8,128)(2,1)S(1)}, bf16[2048,512]{1,0:T(8,128)(2,1)S(1)}, u32[]{:S(2)}, u32[]{:S(2)}) collective-permute-start(bf16[2048,512]{1,0:T(8,128)(2,1)S(1)} %copy-done.31), channel_id=1, source_target_pairs={{0,1},{1,0},{2,3},{3,2},{4,5},{5,4},{6,7},{7,6}} | collective-permute-start | bytes 6291464 | tf_op jit(solution)/shard_map/ppermute | solution.py:676
  490.4 13.3 %slice-start = ((s8[8388608]{0:T(1024)(128)(4,1)}), s8[4194304]{0:T(1024)(128)(4,1)S(1)}, s32[]{:S(2)}) async-start(s8[8388608]{0:T(1024)(128)(4,1)} %bitcast.104), calls=%async_computation | async-start | bytes 8388608
  490.4 13.3 %slice-start.1 = ((s8[8388608]{0:T(1024)(128)(4,1)}), s8[4194304]{0:T(1024)(128)(4,1)S(1)}, s32[]{:S(2)}) async-start(s8[8388608]{0:T(1024)(128)(4,1)} %bitcast.104), calls=%async_computation.1 | async-start | bytes 8388608
  490.4 34.8 %collective-permute-start.10 = (f32[2048,512]{1,0:T(8,128)S(1)}, f32[2048,512]{1,0:T(8,128)S(1)}, u32[]{:S(2)}, u32[]{:S(2)}) collective-permute-start(f32[2048,512]{1,0:T(8,128)S(1)} %copy-done.28), channel_id=1, source_target_pairs={{0,1},{1,0},{2,3},{3,2},{4,5},{5,4},{6,7},{7,6}} | collective-permute-start | bytes 12582920 | tf_op jit(solution)/shard_map/ppermute | solution.py:676
  503.7 15.7 %slice-start.2 = ((s8[8388608]{0:T(1024)(128)(4,1)}), s8[4194304]{0:T(1024)(128)(4,1)S(1)}, s32[]{:S(2)}) async-start(s8[8388608]{0:T(1024)(128)(4,1)} %bitcast.126), calls=%async_computation.2 | async-start | bytes 8388608
  503.7 15.7 %slice-start.3 = ((s8[8388608]{0:T(1024)(128)(4,1)}), s8[4194304]{0:T(1024)(128)(4,1)S(1)}, s32[]{:S(2)}) async-start(s8[8388608]{0:T(1024)(128)(4,1)} %bitcast.126), calls=%async_computation.3 | async-start | bytes 8388608
  511.8 7.6 %copy-start.35 = (bf16[2048,512]{1,0:T(8,128)(2,1)S(1)}, bf16[2048,512]{1,0:T(8,128)(2,1)}, u32[]{:S(2)}) copy-start(bf16[2048,512]{1,0:T(8,128)(2,1)} %get-tuple-element.83) | copy-start | bytes 6291460
  525.2 2.1 copy-start.29
  528.5 48.9 %copy-start.8 = (bf16[1024,1152]{1,0:T(8,128)(2,1)S(1)}, bf16[1024,1152]{1,0:T(8,128)(2,1)}, u32[]{:S(2)}) copy-start(bf16[1024,1152]{1,0:T(8,128)(2,1)} %copy-done.7) | copy-start | bytes 7077892
  572.8 22.5 %collective-permute-start.11 = (bf16[2048,2048]{1,0:T(8,128)(2,1)}, bf16[2048,2048]{1,0:T(8,128)(2,1)}, u32[]{:S(2)}, u32[]{:S(2)}) collective-permute-start(bf16[2048,2048]{1,0:T(8,128)(2,1)} %get-tuple-element.91.mine0.mine1), channel_id=1, source_target_pairs={{0,1},{1,0},{2,3},{3,2},{4,5},{5,4},{6,7},{7,6}} | collective-permute-start | bytes 25165832 | tf_op jit(solution)/shard_map/ppermute | solution.py:676
  574.6 13.3 %collective-permute-start.19 = (bf16[2048,256]{1,0:T(8,128)(2,1)S(1)}, bf16[2048,256]{1,0:T(8,128)(2,1)}, u32[]{:S(2)}, u32[]{:S(2)}) collective-permute-start(bf16[2048,256]{1,0:T(8,128)(2,1)S(1)} %broadcast_select_fusion.2), channel_id=1, source_target_pairs={{0,1},{1,0},{2,3},{3,2},{4,5},{5,4},{6,7},{7,6}} | collective-permute-start | bytes 3145736 | tf_op jit(solution)/shard_map/ppermute | solution.py:676
  577.4 45.2 %collective-permute-start.13 = (bf16[1024,1152]{1,0:T(8,128)(2,1)S(1)}, bf16[1024,1152]{1,0:T(8,128)(2,1)}, u32[]{:S(2)}, u32[]{:S(2)}) collective-permute-start(bf16[1024,1152]{1,0:T(8,128)(2,1)S(1)} %copy-done.8), channel_id=1, source_target_pairs={{0,1},{1,0},{2,3},{3,2},{4,5},{5,4},{6,7},{7,6}} | collective-permute-start | bytes 7077896 | tf_op jit(solution)/shard_map/ppermute | solution.py:676
  577.8 59.4 %collective-permute-start.21 = (bf16[512,2048]{1,0:T(8,128)(2,1)}, bf16[512,2048]{1,0:T(8,128)(2,1)}, u32[]{:S(2)}, u32[]{:S(2)}) collective-permute-start(bf16[512,2048]{1,0:T(8,128)(2,1)} %add_convert_fusion.2.refs_0_), channel_id=1, source_target_pairs={{0,3},{1,2},{2,1},{3,0},{4,7},{5,6},{6,5},{7,4}} | collective-permute-start | bytes 6291464 | tf_op jit(solution)/shard_map/ppermute | solution.py:673
  578.4 92.2 %collective-permute-start.16 = (bf16[2048,512]{1,0:T(8,128)(2,1)}, bf16[2048,512]{1,0:T(8,128)(2,1)}, u32[]{:S(2)}, u32[]{:S(2)}) collective-permute-start(bf16[2048,512]{1,0:T(8,128)(2,1)} %add_convert_fusion.1.refs_0_), channel_id=1, source_target_pairs={{0,3},{1,2},{2,1},{3,0},{4,7},{5,6},{6,5},{7,4}} | collective-permute-start | bytes 6291464 | tf_op jit(solution)/shard_map/ppermute | solution.py:673
  595.4 12.0 %copy-start.11 = (bf16[2048,256]{1,0:T(8,128)(2,1)S(1)}, bf16[2048,256]{1,0:T(8,128)(2,1)}, u32[]{:S(2)}) copy-start(bf16[2048,256]{1,0:T(8,128)(2,1)} %get-tuple-element.101) | copy-start | bytes 3145732
  606.6 7.8 %slice-start.4 = ((s8[4718592]{0:T(1024)(128)(4,1)}), s8[4194304]{0:T(1024)(128)(4,1)S(1)}, s32[]{:S(2)}) async-start(s8[4718592]{0:T(1024)(128)(4,1)} %bitcast.128), calls=%async_computation.4 | async-start | bytes 8388608
  606.6 7.8 %copy-start.2 = (bf16[512,1152]{1,0:T(8,128)(2,1)S(1)}, bf16[512,1152]{1,0:T(8,128)(2,1)}, u32[]{:S(2)}) copy-start(bf16[512,1152]{1,0:T(8,128)(2,1)} %pool.1) | copy-start | bytes 3538948
  606.6 7.8 %copy-start.4 = (bf16[512,1152]{1,0:T(8,128)(2,1)S(1)}, bf16[512,1152]{1,0:T(8,128)(2,1)}, u32[]{:S(2)}) copy-start(bf16[512,1152]{1,0:T(8,128)(2,1)} %copy-done.3) | copy-start | bytes 3538948
  606.7 7.8 %copy-start.13 = (f32[1152]{0:T(1024)S(1)}, f32[1152]{0:T(1024)}, u32[]{:S(2)}) copy-start(f32[1152]{0:T(1024)} %copy-done.12) | copy-start | bytes 13828
  606.7 7.7 %copy-start.17 = (f32[1024]{0:T(1024)S(1)}, f32[1024]{0:T(1024)}, u32[]{:S(2)}) copy-start(f32[1024]{0:T(1024)} %copy-done.16) | copy-start | bytes 12292
  606.7 7.7 %slice-start.5 = ((s8[4718592]{0:T(1024)(128)(4,1)}), s8[524288]{0:T(1024)(128)(4,1)S(1)}, s32[]{:S(2)}) async-start(s8[4718592]{0:T(1024)(128)(4,1)} %bitcast.128), calls=%async_computation.5 | async-start | bytes 1048576
  606.7 7.7 %copy-start.30 = (bf16[1024,2048]{1,0:T(8,128)(2,1)S(1)}, bf16[1024,2048]{1,0:T(8,128)(2,1)}, u32[]{:S(2)}) copy-start(bf16[1024,2048]{1,0:T(8,128)(2,1)} %get-tuple-element.92) | copy-start | bytes 12582916
  606.7 16.3 %collective-permute-start.14 = (bf16[1024,1024]{1,0:T(8,128)(2,1)}, bf16[1024,1024]{1,0:T(8,128)(2,1)}, u32[]{:S(2)}, u32[]{:S(2)}) collective-permute-start(bf16[1024,1024]{1,0:T(8,128)(2,1)} %get-tuple-element.98), channel_id=1, source_target_pairs={{0,1},{1,0},{2,3},{3,2},{4,5},{5,4},{6,7},{7,6}} | collective-permute-start | bytes 6291464 | tf_op jit(solution)/shard_map/ppermute | solution.py:676
  614.2 56.5 %collective-permute-start.20 = (bf16[2048,256]{1,0:T(8,128)(2,1)S(1)}, bf16[2048,256]{1,0:T(8,128)(2,1)S(1)}, u32[]{:S(2)}, u32[]{:S(2)}) collective-permute-start(bf16[2048,256]{1,0:T(8,128)(2,1)S(1)} %fusion.7), channel_id=1, source_target_pairs={{0,1},{1,0},{2,3},{3,2},{4,5},{5,4},{6,7},{7,6}} | collective-permute-start | bytes 3145736 | tf_op jit(solution)/shard_map/ppermute | solution.py:676
  614.5 8.0 %copy-start.21 = (f32[1,2048]{1,0:T(1,128)S(1)}, f32[1,2048]{1,0:T(1,128)}, u32[]{:S(2)}) copy-start(f32[1,2048]{1,0:T(1,128)} %get-tuple-element.93) | copy-start | bytes 24580
  614.5 8.0 %copy-start.25 = (f32[1,256]{1,0:T(1,128)S(1)}, f32[1,256]{1,0:T(1,128)}, u32[]{:S(2)}) copy-start(f32[1,256]{1,0:T(1,128)} %get-tuple-element.94) | copy-start | bytes 3076
  614.5 8.0 %copy-start.26 = (f32[1,256]{1,0:T(1,128)S(1)}, f32[1,256]{1,0:T(1,128)}, u32[]{:S(2)}) copy-start(f32[1,256]{1,0:T(1,128)} %get-tuple-element.95) | copy-start | bytes 3076
  614.5 8.0 %copy-start.20 = (f32[1,2048]{1,0:T(1,128)S(1)}, f32[1,2048]{1,0:T(1,128)}, u32[]{:S(2)}) copy-start(f32[1,2048]{1,0:T(1,128)} %get-tuple-element.96) | copy-start | bytes 24580
  614.5 8.0 %copy-start.19 = (f32[1024]{0:T(1024)S(1)}, f32[1024]{0:T(1024)}, u32[]{:S(2)}) copy-start(f32[1024]{0:T(1024)} %copy-done.18) | copy-start | bytes 12292
  622.6 5.6 copy-start.32
  622.6 48.6 %collective-permute-start.12 = (f32[5760]{0:T(1024)S(1)}, f32[5760]{0:T(1024)S(1)}, u32[]{:S(2)}, u32[]{:S(2)}) collective-permute-start(f32[5760]{0:T(1024)S(1)} %constant_dynamic-update-slice_fusion), channel_id=1, source_target_pairs={{0,1},{1,0},{2,3},{3,2},{4,5},{5,4},{6,7},{7,6}} | collective-permute-start | bytes 69128 | tf_op jit(solution)/shard_map/ppermute | solution.py:676
  632.2 74.1 %collective-permute-start.15 = (bf16[1152,1024]{1,0:T(8,128)(2,1)}, bf16[1152,1024]{1,0:T(8,128)(2,1)S(1)}, u32[]{:S(2)}, u32[]{:S(2)}) collective-permute-start(bf16[1152,1024]{1,0:T(8,128)(2,1)} %add_convert_fusion.refs_0_), channel_id=1, source_target_pairs={{0,1},{1,0},{2,3},{3,2},{4,5},{5,4},{6,7},{7,6}} | collective-permute-start | bytes 7077896 | tf_op jit(solution)/shard_map/ppermute | solution.py:676
  637.2 47.6 %collective-permute-start.22 = (bf16[512,2048]{1,0:T(8,128)(2,1)}, bf16[512,2048]{1,0:T(8,128)(2,1)}, u32[]{:S(2)}, u32[]{:S(2)}) collective-permute-start(bf16[512,2048]{1,0:T(8,128)(2,1)} %add_convert_fusion.2.refs_0_), channel_id=1, source_target_pairs={{0,1},{1,0},{2,3},{3,2},{4,5},{5,4},{6,7},{7,6}} | collective-permute-start | bytes 6291464 | tf_op jit(solution)/shard_map/ppermute | solution.py:676
  670.6 24.9 %collective-permute-start.17 = (bf16[2048,512]{1,0:T(8,128)(2,1)}, bf16[2048,512]{1,0:T(8,128)(2,1)}, u32[]{:S(2)}, u32[]{:S(2)}) collective-permute-start(bf16[2048,512]{1,0:T(8,128)(2,1)} %add_convert_fusion.1.refs_0_), channel_id=1, source_target_pairs={{0,1},{1,0},{2,3},{3,2},{4,5},{5,4},{6,7},{7,6}} | collective-permute-start | bytes 6291464 | tf_op jit(solution)/shard_map/ppermute | solution.py:676
  670.8 14.0 %collective-permute-start.23 = (bf16[512,2048]{1,0:T(8,128)(2,1)}, bf16[512,2048]{1,0:T(8,128)(2,1)}, u32[]{:S(2)}, u32[]{:S(2)}) collective-permute-start(bf16[512,2048]{1,0:T(8,128)(2,1)} %collective-permute-done.21.refs_1_), channel_id=1, source_target_pairs={{0,1},{1,0},{2,3},{3,2},{4,5},{5,4},{6,7},{7,6}} | collective-permute-start | bytes 6291464 | tf_op jit(solution)/shard_map/ppermute | solution.py:676
  671.2 24.4 %collective-permute-start.18 = (bf16[2048,512]{1,0:T(8,128)(2,1)}, bf16[2048,512]{1,0:T(8,128)(2,1)}, u32[]{:S(2)}, u32[]{:S(2)}) collective-permute-start(bf16[2048,512]{1,0:T(8,128)(2,1)} %collective-permute-done.16.refs_1_), channel_id=1, source_target_pairs={{0,1},{1,0},{2,3},{3,2},{4,5},{5,4},{6,7},{7,6}} | collective-permute-start | bytes 6291464 | tf_op jit(solution)/shard_map/ppermute | solution.py:676
  706.3 1.4 copy-start.9
  (2 other events, 1.9 us)
